TPU v7x, 128 devices: a whole 4x4x4 slice. The times are simulated.
128 devices in a mesh: gz: 16 (over z, y), gy: 8 (over x, core).
Axes of the slice: x: 4, y: 4, z: 4, core: 2. Of those that a mesh axis runs over, the one named last changes fastest.
Arguments:
- density: float32 [128, 123904], P('gz', 'gy'), may hold values from -6 to 6
Outputs:
- potential: float32 [128, 123904], P('gz', 'gy')
All inputs are finite; a program needn't handle non-finite values.
Results may differ from a plain program's by a relative error of at most 0.00014.
Values sent between devices are 32-bit elements; how exact they have to be, the bound alone decides.
No kernel may reach another device: no remote copies, remote signals or barrier semaphores. Data moves between devices by JAX's collectives and lax.ppermute only.
A program may use at most 64 MiB of HBM per device.

v0:
```python
import math

import jax
import jax.numpy as jnp
import numpy as np
from jax import lax
from jax.experimental import pallas as pl
from jax.experimental.pallas import tpu as pltpu
from jax.sharding import PartitionSpec as P

NX = 352
NY = 352
SCREEN = 128
TWO_PI = 2.0 * math.pi

PAD = 384
LANES = 128
TILES = PAD // LANES
GZ = 16
GY = 8
PLANES = 8
ROWS = NY // GY
CHUNK = PAD // GY
OWN = 3
PEERS = GZ * GY
SEND = PEERS * OWN * TILES
BELONG = OWN * TILES

F32 = jnp.float32
BF16 = jnp.bfloat16


def real_basis(length):
    index = np.arange(length)
    basis = np.zeros((length, length))
    for row in range(length):
        m = (row + 1) // 2
        angle = 2.0 * np.pi * ((m * index) % length) / length
        wave = np.cos(angle) if row % 2 == 1 or row == 0 else np.sin(angle)
        weight = 1.0 if row == 0 or row == length - 1 else 2.0
        basis[row] = wave * np.sqrt(weight / length)
    return basis


def halves(table):
    single = table.astype(np.float32)
    high = single.astype(jnp.bfloat16)
    low = (single - high.astype(np.float32)).astype(jnp.bfloat16)
    return high, low


def x_table():
    table = np.zeros((PAD, PAD))
    table[:NX, :NX] = real_basis(NX)
    return halves(table)


def y_table():
    table = np.zeros((PAD, GY, CHUNK))
    table[:NY, :, :ROWS] = real_basis(NY).reshape(NY, GY, ROWS)
    return halves(table.reshape(PAD, PAD))


def split(value):
    high = value.astype(BF16)
    return high, (value - high.astype(F32)).astype(BF16)


def product(left, right, dims):
    def dot(a, b):
        return lax.dot_general(a, b, (dims, ((), ())), preferred_element_type=F32)

    return dot(left[0], right[0]) + (dot(left[0], right[1]) + dot(left[1], right[0]))


def lane_tile(j):
    return slice(j * LANES, (j + 1) * LANES)


def forward_x(x_ref, high_ref, low_ref, out_ref, field_ref):
    for y in range(CHUNK):
        if y < ROWS:
            offset = y * NX
            shift = offset % LANES
            width = PAD if shift <= PAD - NX else PAD + LANES
            value = x_ref[:, pl.ds(offset - shift, width)]
            if shift:
                value = pltpu.roll(value, width - shift, 1)
        else:
            value = jnp.zeros((PLANES, PAD), F32)
        for j in range(TILES):
            field_ref[j, pl.ds(y, PLANES, stride=CHUNK), :] = value[:, lane_tile(j)]
    field = jnp.concatenate([field_ref[j] for j in range(TILES)], axis=1)
    result = product((high_ref[...], low_ref[...]), split(field), ((1,), (1,)))
    for j in range(TILES):
        out_ref[pl.ds(j, PAD, stride=TILES), :] = result[:, lane_tile(j)]


def chunk_pick(parts, lane):
    out = []
    for j in range(TILES):
        first = j * LANES // CHUNK
        last = ((j + 1) * LANES - 1) // CHUNK
        value = parts[last][j]
        for c in range(last - 1, first - 1, -1):
            value = jnp.where(lane < (c + 1) * CHUNK - j * LANES, parts[c][j], value)
        out.append(value)
    return out


def swap_chunks(arrays, lane):
    turned = []
    for d in range(GY):
        picked = chunk_pick([arrays[(c + d) % GY] for c in range(GY)], lane)
        whole = jnp.concatenate(picked, axis=1)
        if d:
            whole = pltpu.roll(whole, CHUNK * d, 1)
        turned.append([whole[:, lane_tile(j)] for j in range(TILES)])
    return [chunk_pick([turned[(c - b) % GY] for c in range(GY)], lane) for b in range(GY)]


def middle(in_ref, high_ref, low_ref, decay_ref, scale_ref, out_ref, work_ref, phi_ref):
    lane = lax.broadcasted_iota(jnp.int32, (8, LANES), 1)
    block = OWN * GZ
    for tile in range(block // 8):
        own, half = divmod(tile, GZ // 8)
        arrays = [
            [
                in_ref[pl.ds((half * 8 * GY + g) * BELONG + own * TILES + j, 8, stride=GY * BELONG), :]
                for j in range(TILES)
            ]
            for g in range(GY)
        ]
        for z, parts in enumerate(swap_chunks(arrays, lane)):
            for j in range(TILES):
                work_ref[pl.ds(z * block + tile * 8, 8), lane_tile(j)] = parts[j]
    table = (high_ref[...], low_ref[...])
    phi_ref[...] = product(split(work_ref[...]), table, ((1,), (1,)))

    gz = lax.broadcasted_iota(jnp.int32, (GZ, LANES), 0)
    for own in range(OWN):
        for j in range(TILES):
            decay = decay_ref[pl.ds(own, 1), lane_tile(j)]
            scale = scale_ref[pl.ds(own, 1), lane_tile(j)]
            decay = jnp.broadcast_to(decay, (GZ, LANES))
            scale = jnp.broadcast_to(scale, (GZ, LANES))
            hat = [phi_ref[pl.ds(z * block + own * GZ, GZ), lane_tile(j)] for z in range(PLANES)]
            up = [hat[0]]
            for z in range(1, PLANES):
                up.append(decay * up[-1] + hat[z])
            down = [jnp.zeros((GZ, LANES), F32)]
            for z in range(PLANES - 1, 0, -1):
                down.append(decay * (down[-1] + hat[z]))
            down = down[::-1]
            over = up[-1]
            under = decay * (down[0] + hat[0])
            power = decay * decay
            power = power * power
            power = power * power
            step = 1
            while step < GZ:
                over = over + jnp.where(gz >= step, power * pltpu.roll(over, step, 0), 0.0)
                under = under + jnp.where(gz < GZ - step, power * pltpu.roll(under, GZ - step, 0), 0.0)
                power = power * power
                step *= 2
            over = jnp.where(gz >= 1, pltpu.roll(over, 1, 0), 0.0)
            under = jnp.where(gz < GZ - 1, pltpu.roll(under, GZ - 1, 0), 0.0)
            for z in range(PLANES):
                over = decay * over
                up[z] = up[z] + over
            for z in range(PLANES - 1, -1, -1):
                down[z] = down[z] + under
                under = decay * under
            for z in range(PLANES):
                phi_ref[pl.ds(z * block + own * GZ, GZ), lane_tile(j)] = (up[z] + down[z]) * scale

    work_ref[...] = product(split(phi_ref[...]), table, ((1,), (0,)))
    for tile in range(block // 8):
        own, half = divmod(tile, GZ // 8)
        arrays = [
            [work_ref[pl.ds(z * block + tile * 8, 8), lane_tile(j)] for j in range(TILES)] for z in range(PLANES)
        ]
        for g, parts in enumerate(swap_chunks(arrays, lane)):
            for j in range(TILES):
                out_ref[pl.ds((half * 8 * GY + g) * BELONG + own * TILES + j, 8, stride=GY * BELONG), :] = parts[j]


def backward_x(in_ref, high_ref, low_ref, out_ref, field_ref):
    value = jnp.concatenate([in_ref[pl.ds(j, PAD, stride=TILES), :] for j in range(TILES)], axis=1)
    table = (high_ref[...], low_ref[...])
    result = product(split(jnp.transpose(value)), table, ((1,), (0,)))
    for j in range(TILES):
        field_ref[j] = result[:, lane_tile(j)]
    carry = None
    for y in range(ROWS):
        offset = y * NX
        shift = offset % LANES
        value = jnp.concatenate([field_ref[j, pl.ds(y, PLANES, stride=CHUNK), :] for j in range(TILES)], axis=1)
        if shift > PAD - NX:
            value = jnp.concatenate([value, jnp.zeros((PLANES, LANES), F32)], axis=1)
        if shift:
            value = pltpu.roll(value, shift, 1)
        tiles = [value[:, lane_tile(j)] for j in range(value.shape[1] // LANES)]
        if carry is not None:
            tiles[0] = tiles[0] + carry
        end = shift + NX
        full = end // LANES
        carry = tiles[full] if end % LANES else None
        for j in range(full):
            out_ref[:, pl.ds(offset - shift + j * LANES, LANES)] = tiles[j]


def call(kernel, out_shape, scratch, *args):
    return pl.pallas_call(
        kernel,
        out_shape=jax.ShapeDtypeStruct(out_shape, F32),
        in_specs=[pl.BlockSpec(memory_space=pltpu.VMEM)] * len(args),
        out_specs=pl.BlockSpec(memory_space=pltpu.VMEM),
        scratch_shapes=[pltpu.VMEM(shape, F32) for shape in scratch],
    )(*args)


def wavenumber(index, length):
    return ((index + 1) // 2).astype(F32) * (TWO_PI / length)


def exchange(buffer):
    return lax.all_to_all(buffer, ("gz", "gy"), 0, 0, tiled=True)


def on_device(density):
    x_high, x_low = (jnp.asarray(t) for t in x_table())
    y_high, y_low = (jnp.asarray(t) for t in y_table())
    own = lax.axis_index("gz") * GY + lax.axis_index("gy")
    index_x = jnp.minimum(own * OWN + jnp.arange(OWN, dtype=jnp.int32), NX - 1)
    index_y = jnp.minimum(jnp.arange(PAD, dtype=jnp.int32), NY - 1)
    wave_x = wavenumber(index_x, NX)
    wave_y = wavenumber(index_y, NY)
    kappa = jnp.sqrt(1.0 / (SCREEN * SCREEN) + wave_x[:, None] ** 2 + wave_y[None, :] ** 2)
    decay = jnp.exp(-kappa)
    scale = 0.5 / kappa

    field = [(TILES, PAD, LANES)]
    sent = call(forward_x, (SEND, LANES), field, density, x_high, x_low)
    held = exchange(sent)
    back = call(middle, (SEND, LANES), [(PAD, PAD)] * 2, held, y_high, y_low, decay, scale)
    held = exchange(back)
    return call(backward_x, density.shape, field, held, x_high, x_low)


def solution(mesh):
    return jax.shard_map(
        on_device,
        mesh=mesh,
        in_specs=(P("gz", "gy"),),
        out_specs=P("gz", "gy"),
        check_vma=False,
    )
```

profile of v0, /device:TPU:1, one launch (start us, length us, event | category | flops | bytes accessed | tf_op | source)
XLA Modules:
  0.0 69.4 jit_solution(3965589953736839907)
XLA Ops:
  0.0 3.0 %shard_map.55 = f32[1152,128]{1,0:T(8,128)} custom-call(f32[8,15488]{1,0:T(8,128)} %x_ref.1, bf16[384,384]{1,0:T(8,128)(2,1)} %constant.56.clone.high_ref, bf16[384,384]{1,0:T(8,128)(2,1)} %constant.57.clone.low_ref), custom_call_target="tpu_custom_call" | custom-call | tf_op jit(solution)/shard_map/pallas_call | solution.py:214
  3.0 2.1 %all_to_all.14 = f32[128,9,128]{2,1,0:T(8,128)} reshape(f32[1152,128]{1,0:T(8,128)} %shard_map.55) | data formatting | bytes 1179648 | tf_op jit(solution)/shard_map/all_to_all | solution.py:228
  5.1 11.5 %all-to-all-start = ((f32[128,9,128]{2,1,0:T(8,128)}), f32[128,9,128]{2,1,0:T(8,128)S(1)}, u32[]{:S(2)}, u32[]{:S(2)}) async-start(f32[128,9,128]{2,1,0:T(8,128)} %all_to_all.14), calls=%async_computation | async-start | bytes 2097152 | tf_op jit(solution)/shard_map/all_to_all | solution.py:228
  16.6 0.7 fusion
  17.3 18.5 %all-to-all-done = f32[128,9,128]{2,1,0:T(8,128)S(1)} async-done(((f32[128,9,128]{2,1,0:T(8,128)}), f32[128,9,128]{2,1,0:T(8,128)S(1)}, u32[]{:S(2)}, u32[]{:S(2)}) %all-to-all-start) | async-done | bytes 589856 | tf_op jit(solution)/shard_map/all_to_all | solution.py:228
  35.8 0.9 %all_to_all.16.in_ref = f32[1152,128]{1,0:T(8,128)} reshape(f32[128,9,128]{2,1,0:T(8,128)S(1)} %all-to-all-done) | data formatting | bytes 1179648 | tf_op jit(solution)/shard_map/all_to_all | solution.py:228
  36.7 4.2 %shard_map.56 = f32[1152,128]{1,0:T(8,128)} custom-call(f32[1152,128]{1,0:T(8,128)} %all_to_all.16.in_ref, bf16[384,384]{1,0:T(8,128)(2,1)} %constant.58.clone.high_ref, bf16[384,384]{1,0:T(8,128)(2,1)} %constant.59.clone.low_ref, f32[3,384]{1,0:T(4,128)} %get-tuple-element.6.decay_ref, f32[3,384]{1,0:T(4,128)} %get-tuple-element.5.scale_ref), custom_call_target="tpu_custom_call" | custom-call | tf_op jit(solution)/shard_map/pallas_call | solution.py:214
  40.9 1.1 %all_to_all.17 = f32[128,9,128]{2,1,0:T(8,128)S(1)} reshape(f32[1152,128]{1,0:T(8,128)} %shard_map.56) | data formatting | bytes 1179648 | tf_op jit(solution)/shard_map/all_to_all | solution.py:228
  42.0 23.5 %all_to_all.22 = f32[128,9,128]{2,1,0:T(8,128)S(1)} all-to-all(f32[128,9,128]{2,1,0:T(8,128)S(1)} %all_to_all.17), channel_id=1, replica_groups=mesh['gz'=16,'gy'=8] {'gz','gy'}, dimensions={0} | all-to-all | bytes 1179648 | tf_op jit(solution)/shard_map/all_to_all | solution.py:228
  65.5 0.9 %all_to_all.19.in_ref = f32[1152,128]{1,0:T(8,128)} reshape(f32[128,9,128]{2,1,0:T(8,128)S(1)} %all_to_all.22) | data formatting | bytes 1179648 | tf_op jit(solution)/shard_map/all_to_all | solution.py:228
  66.4 3.0 %shard_map.57 = f32[8,15488]{1,0:T(8,128)} custom-call(f32[1152,128]{1,0:T(8,128)} %all_to_all.19.in_ref, bf16[384,384]{1,0:T(8,128)(2,1)} %constant.56.clone.high_ref, bf16[384,384]{1,0:T(8,128)(2,1)} %constant.57.clone.low_ref), custom_call_target="tpu_custom_call" | custom-call | tf_op jit(solution)/shard_map/pallas_call | solution.py:214
  (2 shorter events, 0.0 us)
Async XLA Ops:
  5.1 30.7 %all-to-all-start = ((f32[128,9,128]{2,1,0:T(8,128)}), f32[128,9,128]{2,1,0:T(8,128)S(1)}, u32[]{:S(2)}, u32[]{:S(2)}) async-start(f32[128,9,128]{2,1,0:T(8,128)} %all_to_all.14), calls=%async_computation | async-start | bytes 2097152 | tf_op jit(solution)/shard_map/all_to_all | solution.py:228
where the time goes:
time: 69.7 us; the launch traced here: 69.4 us
  blocking collectives  23.5 us (34%)
  waiting for transfers between devices  18.5 us (27%)
  starting transfers between devices  11.5 us (16%)
  Pallas kernels  10.2 us (15%)
  local copies, waits for them, and re-layouts  4.99 us (7%)
  other arithmetic  0.71 us (1%)
    all_to_all x1, blocking collectives, exchange(): return lax.all_to_all(buffer, ('gz', 'gy'), 0, 0, tiled=True)  23.5 us
    all_to_all x1, waiting for transfers between devices, exchange(): return lax.all_to_all(buffer, ('gz', 'gy'), 0, 0, tiled=True)  18.5 us
    all_to_all x1, starting transfers between devices, exchange(): return lax.all_to_all(buffer, ('gz', 'gy'), 0, 0, tiled=True)  11.5 us
    pallas_call x3, Pallas kernels, call(): pl.pallas_call(kernel, out_shape=jax.ShapeDtypeStruct(out_shape, F32), in...  10.2 us
    all_to_all x4, local copies, waits for them, and re-layouts, exchange(): return lax.all_to_all(buffer, ('gz', 'gy'), 0, 0, tiled=True)  4.99 us
  transfers between devices with their start and end apart: 1, of which 1 were waited for; matrix products, arithmetic and copies ran while one was open for 1% of the time, Pallas kernels for 0%

commit v1 on v0

--- a/solution.py
+++ b/solution.py
@@ -225,7 +225,9 @@
 
 
 def exchange(buffer):
-    return lax.all_to_all(buffer, ("gz", "gy"), 0, 0, tiled=True)
+    whole = buffer.reshape(PEERS, 1, BELONG * LANES)
+    whole = lax.all_to_all(whole, ("gz", "gy"), 0, 0, tiled=True)
+    return whole.reshape(SEND, LANES)
 
 
 def on_device(density):

time: 69.7 us -> 56.8 us (0.81)
  waiting for transfers between devices: 18.5 us -> 13.6 us
  local copies, waits for them, and re-layouts: 4.99 us -> 0.82 us
  blocking collectives: 23.5 us -> 19.7 us
    all_to_all x4 -> x0, local copies, waits for them, and re-layouts: 4.99 us -> none  [exchange(): return lax.all_to_all(buffer, ('gz', 'gy'), 0, 0, tiled=True)]
    all_to_all x1, waiting for transfers between devices: 18.5 us -> 13.6 us  [exchange(): whole = lax.all_to_all(whole, ('gz', 'gy'), 0, 0, tiled=True)]
    all_to_all x1, blocking collectives: 23.5 us -> 19.7 us  [exchange(): whole = lax.all_to_all(whole, ('gz', 'gy'), 0, 0, tiled=True)]
    unnamed x0 -> x2, local copies, waits for them, and re-layouts: none -> 0.82 us
where the time goes in v1:
time: 56.8 us; the launch traced here: 56.6 us
  blocking collectives  19.7 us (35%)
  waiting for transfers between devices  13.6 us (24%)
  starting transfers between devices  11.5 us (20%)
  Pallas kernels  10.2 us (18%)
  local copies, waits for them, and re-layouts  0.82 us (1%)
  other arithmetic  0.71 us (1%)
    all_to_all x1, blocking collectives, exchange(): whole = lax.all_to_all(whole, ('gz', 'gy'), 0, 0, tiled=True)  19.7 us
    all_to_all x1, waiting for transfers between devices, exchange(): whole = lax.all_to_all(whole, ('gz', 'gy'), 0, 0, tiled=True)  13.6 us
    all_to_all x1, starting transfers between devices, exchange(): whole = lax.all_to_all(whole, ('gz', 'gy'), 0, 0, tiled=True)  11.5 us
    pallas_call x3, Pallas kernels, call(): pl.pallas_call(kernel, out_shape=jax.ShapeDtypeStruct(out_shape, F32), in...  10.2 us
  transfers between devices with their start and end apart: 1, of which 1 were waited for; matrix products, arithmetic and copies ran while one was open for 1% of the time, Pallas kernels for 0%

profile of v1, /device:TPU:1, one launch (start us, length us, event | category | flops | bytes accessed | tf_op | source)
XLA Modules:
  0.0 56.6 jit_solution(7425225965657587329)
XLA Ops:
  0.0 3.0 %shard_map.55 = f32[1152,128]{1,0:T(8,128)} custom-call(f32[8,15488]{1,0:T(8,128)} %x_ref.1, bf16[384,384]{1,0:T(8,128)(2,1)} %constant.56.clone.high_ref, bf16[384,384]{1,0:T(8,128)(2,1)} %constant.57.clone.low_ref), custom_call_target="tpu_custom_call" | custom-call | tf_op jit(solution)/shard_map/pallas_call | solution.py:214
  3.0 11.5 %all-to-all-start = ((f32[128,1,1152]{2,1,0:T(1,128)}), f32[128,1,1152]{2,1,0:T(1,128)S(1)}, u32[]{:S(2)}, u32[]{:S(2)}) async-start(f32[128,1,1152]{2,1,0:T(1,128)} %bitcast.5), calls=%async_computation | async-start | bytes 1179648 | tf_op jit(solution)/shard_map/all_to_all | solution.py:229
  14.5 0.7 %fusion = (f32[3,384]{1,0:T(4,128)}, f32[3,384]{1,0:T(4,128)}) fusion(f32[384]{0:T(512)S(1)} %fusion.4, f32[3]{0:T(128)S(1)} %multiply_add_fusion), kind=kLoop, calls=%fused_computation.2 | loop fusion | flops 3456 | bytes 10764 | tf_op jit(solution)/shard_map/div | solution.py:243
  15.2 13.6 %all-to-all-done = f32[128,1,1152]{2,1,0:T(1,128)S(1)} async-done(((f32[128,1,1152]{2,1,0:T(1,128)}), f32[128,1,1152]{2,1,0:T(1,128)S(1)}, u32[]{:S(2)}, u32[]{:S(2)}) %all-to-all-start) | async-done | bytes 589856 | tf_op jit(solution)/shard_map/all_to_all | solution.py:229
  28.8 0.0 copy-start
  28.8 0.8 %copy-done = f32[128,1,1152]{2,1,0:T(1,128)} copy-done((f32[128,1,1152]{2,1,0:T(1,128)}, f32[128,1,1152]{2,1,0:T(1,128)S(1)}, u32[]{:S(2)}) %copy-start) | copy-done | bytes 589848
  29.6 4.2 %shard_map.56 = f32[1152,128]{1,0:T(8,128)} custom-call(f32[1152,128]{1,0:T(8,128)} %bitcast.4, bf16[384,384]{1,0:T(8,128)(2,1)} %constant.58.clone.high_ref, bf16[384,384]{1,0:T(8,128)(2,1)} %constant.59.clone.low_ref, f32[3,384]{1,0:T(4,128)} %get-tuple-element.6.decay_ref, f32[3,384]{1,0:T(4,128)} %get-tuple-element.5.scale_ref), custom_call_target="tpu_custom_call" | custom-call | tf_op jit(solution)/shard_map/pallas_call | solution.py:214
  33.8 19.7 %all_to_all.10 = f32[128,1,1152]{2,1,0:T(1,128)} all-to-all(f32[128,1,1152]{2,1,0:T(1,128)} %bitcast.6), channel_id=1, replica_groups=mesh['gz'=16,'gy'=8] {'gz','gy'}, dimensions={0} | all-to-all | bytes 1179648 | tf_op jit(solution)/shard_map/all_to_all | solution.py:229
  53.6 3.0 %shard_map.57 = f32[8,15488]{1,0:T(8,128)} custom-call(f32[1152,128]{1,0:T(8,128)} %bitcast.7, bf16[384,384]{1,0:T(8,128)(2,1)} %constant.56.clone.high_ref, bf16[384,384]{1,0:T(8,128)(2,1)} %constant.57.clone.low_ref), custom_call_target="tpu_custom_call" | custom-call | tf_op jit(solution)/shard_map/pallas_call | solution.py:214
  (2 shorter events, 0.0 us)
Async XLA Ops:
  3.0 25.8 %all-to-all-start = ((f32[128,1,1152]{2,1,0:T(1,128)}), f32[128,1,1152]{2,1,0:T(1,128)S(1)}, u32[]{:S(2)}, u32[]{:S(2)}) async-start(f32[128,1,1152]{2,1,0:T(1,128)} %bitcast.5), calls=%async_computation | async-start | bytes 1179648 | tf_op jit(solution)/shard_map/all_to_all | solution.py:229
  28.8 0.8 %copy-start = (f32[128,1,1152]{2,1,0:T(1,128)}, f32[128,1,1152]{2,1,0:T(1,128)S(1)}, u32[]{:S(2)}) copy-start(f32[128,1,1152]{2,1,0:T(1,128)S(1)} %all-to-all-done) | copy-start | bytes 1769476

commit v2 on v1

--- a/solution.py
+++ b/solution.py
@@ -119,7 +119,17 @@
     return [chunk_pick([turned[(c - b) % GY] for c in range(GY)], lane) for b in range(GY)]
 
 
-def middle(in_ref, high_ref, low_ref, decay_ref, scale_ref, out_ref, work_ref, phi_ref):
+def kappa_tile(own, j):
+    device = lax.axis_index("gz") * GY + lax.axis_index("gy")
+    index_x = jnp.minimum(device * OWN + own, NX - 1)
+    lane = lax.broadcasted_iota(jnp.int32, (GZ, LANES), 1)
+    index_y = jnp.minimum(lane + j * LANES, NY - 1)
+    wave_x = jnp.full((GZ, LANES), lax.shift_right_logical(index_x + 1, 1), jnp.int32).astype(F32) * (TWO_PI / NX)
+    wave_y = lax.shift_right_logical(index_y + 1, 1).astype(F32) * (TWO_PI / NY)
+    return jnp.sqrt(1.0 / (SCREEN * SCREEN) + wave_x * wave_x + wave_y * wave_y)
+
+
+def middle(in_ref, high_ref, low_ref, out_ref, work_ref, phi_ref):
     lane = lax.broadcasted_iota(jnp.int32, (8, LANES), 1)
     block = OWN * GZ
     for tile in range(block // 8):
@@ -140,10 +150,9 @@
     gz = lax.broadcasted_iota(jnp.int32, (GZ, LANES), 0)
     for own in range(OWN):
         for j in range(TILES):
-            decay = decay_ref[pl.ds(own, 1), lane_tile(j)]
-            scale = scale_ref[pl.ds(own, 1), lane_tile(j)]
-            decay = jnp.broadcast_to(decay, (GZ, LANES))
-            scale = jnp.broadcast_to(scale, (GZ, LANES))
+            kappa = kappa_tile(own, j)
+            decay = jnp.exp(-kappa)
+            scale = 0.5 / kappa
             hat = [phi_ref[pl.ds(z * block + own * GZ, GZ), lane_tile(j)] for z in range(PLANES)]
             up = [hat[0]]
             for z in range(1, PLANES):
@@ -213,15 +222,11 @@
 def call(kernel, out_shape, scratch, *args):
     return pl.pallas_call(
         kernel,
-        out_shape=jax.ShapeDtypeStruct(out_shape, F32),
+        out_shape=out_shape,
         in_specs=[pl.BlockSpec(memory_space=pltpu.VMEM)] * len(args),
         out_specs=pl.BlockSpec(memory_space=pltpu.VMEM),
         scratch_shapes=[pltpu.VMEM(shape, F32) for shape in scratch],
-    )(*args)
-
-
-def wavenumber(index, length):
-    return ((index + 1) // 2).astype(F32) * (TWO_PI / length)
+    )(*(pltpu.with_memory_space_constraint(a, pltpu.VMEM) for a in args))
 
 
 def exchange(buffer):
@@ -233,21 +238,12 @@
 def on_device(density):
     x_high, x_low = (jnp.asarray(t) for t in x_table())
     y_high, y_low = (jnp.asarray(t) for t in y_table())
-    own = lax.axis_index("gz") * GY + lax.axis_index("gy")
-    index_x = jnp.minimum(own * OWN + jnp.arange(OWN, dtype=jnp.int32), NX - 1)
-    index_y = jnp.minimum(jnp.arange(PAD, dtype=jnp.int32), NY - 1)
-    wave_x = wavenumber(index_x, NX)
-    wave_y = wavenumber(index_y, NY)
-    kappa = jnp.sqrt(1.0 / (SCREEN * SCREEN) + wave_x[:, None] ** 2 + wave_y[None, :] ** 2)
-    decay = jnp.exp(-kappa)
-    scale = 0.5 / kappa
-
     field = [(TILES, PAD, LANES)]
-    sent = call(forward_x, (SEND, LANES), field, density, x_high, x_low)
+    sent = call(forward_x, pltpu.VMEM((SEND, LANES), F32), field, density, x_high, x_low)
     held = exchange(sent)
-    back = call(middle, (SEND, LANES), [(PAD, PAD)] * 2, held, y_high, y_low, decay, scale)
+    back = call(middle, pltpu.VMEM((SEND, LANES), F32), [(PAD, PAD)] * 2, held, y_high, y_low)
     held = exchange(back)
-    return call(backward_x, density.shape, field, held, x_high, x_low)
+    return call(backward_x, jax.ShapeDtypeStruct(density.shape, F32), field, held, x_high, x_low)
 
 
 def solution(mesh):

time: 56.8 us -> 52.5 us (0.924)
  blocking collectives: 19.7 us -> 44.3 us
  waiting for transfers between devices: 13.6 us -> 0 us
  starting transfers between devices: 11.5 us -> 0 us
  Pallas kernels: 10.2 us -> 4.91 us
  local copies, waits for them, and re-layouts: 0.82 us -> 2.98 us
  other arithmetic: 0.71 us -> 0 us
    all_to_all x1 -> x2, blocking collectives: 19.7 us -> 44.3 us  [exchange(): whole = lax.all_to_all(whole, ('gz', 'gy'), 0, 0, tiled=True)]
    all_to_all x1 -> x0, waiting for transfers between devices: 13.6 us -> none  [exchange(): whole = lax.all_to_all(whole, ('gz', 'gy'), 0, 0, tiled=True)]
    all_to_all x1 -> x0, starting transfers between devices: 11.5 us -> none  [exchange(): whole = lax.all_to_all(whole, ('gz', 'gy'), 0, 0, tiled=True)]
    pallas_call x3, Pallas kernels: 10.2 us -> 4.91 us  [call(): pl.pallas_call(kernel, out_shape=out_shape, in_specs=[pl.BlockSpec(memory...]
    unnamed x2 -> x14, local copies, waits for them, and re-layouts: 0.82 us -> 2.98 us
    div x1 -> x0, other arithmetic: 0.69 us -> none  [on_device(): scale = 0.5 / kappa]
  transfers between devices with their start and end apart: 1 -> 0, of which waited for: 1 -> 0; matrix products, arithmetic and copies ran while one was open for 1% -> 0% of each run, Pallas kernels for 0% -> 0%
where the time goes in v2:
time: 52.5 us; the launch traced here: 52.2 us
  blocking collectives  44.3 us (84%)
  Pallas kernels  4.91 us (9%)
  local copies, waits for them, and re-layouts  2.98 us (6%)
    all_to_all x2, blocking collectives, exchange(): whole = lax.all_to_all(whole, ('gz', 'gy'), 0, 0, tiled=True)  44.3 us
    pallas_call x3, Pallas kernels, call(): pl.pallas_call(kernel, out_shape=out_shape, in_specs=[pl.BlockSpec(memory...  4.91 us
    unnamed x14, local copies, waits for them, and re-layouts  2.98 us

profile of v2, /device:TPU:1, one launch (start us, length us, event | category | flops | bytes accessed | tf_op | source)
XLA Modules:
  0.0 52.2 jit_solution(18263962398467512392)
XLA Ops:
  0.0 0.0 copy-start
  0.0 1.0 %copy-done = bf16[384,384]{1,0:T(8,128)(2,1)S(1)} copy-done((bf16[384,384]{1,0:T(8,128)(2,1)S(1)}, bf16[384,384]{1,0:T(8,128)(2,1)}, u32[]{:S(2)}) %copy-start) | copy-done | bytes 294936
  1.0 0.0 copy-start.2
  1.0 1.0 %copy-done.2 = bf16[384,384]{1,0:T(8,128)(2,1)S(1)} copy-done((bf16[384,384]{1,0:T(8,128)(2,1)S(1)}, bf16[384,384]{1,0:T(8,128)(2,1)}, u32[]{:S(2)}) %copy-start.2) | copy-done | bytes 294936
  1.9 0.0 copy-start.4
  1.9 1.0 %copy-done.4 = f32[8,15488]{1,0:T(8,128)S(1)} copy-done((f32[8,15488]{1,0:T(8,128)S(1)}, f32[8,15488]{1,0:T(8,128)}, u32[]{:S(2)}) %copy-start.4) | copy-done | bytes 495640
  3.0 1.0 %shard_map.55 = f32[1152,128]{1,0:T(8,128)S(1)} custom-call(f32[8,15488]{1,0:T(8,128)S(1)} %copy-done.4, bf16[384,384]{1,0:T(8,128)(2,1)S(1)} %copy-done.2, bf16[384,384]{1,0:T(8,128)(2,1)S(1)} %copy-done), custom_call_target="tpu_custom_call" | custom-call | tf_op jit(solution)/shard_map/pallas_call | solution.py:223
  3.9 0.0 copy-start.5
  4.0 0.0 copy-start.6
  4.0 25.6 %all_to_all.10 = f32[128,1,1152]{2,1,0:T(1,128)S(1)} all-to-all(f32[128,1,1152]{2,1,0:T(1,128)S(1)} %bitcast.7), channel_id=1, replica_groups=mesh['gz'=16,'gy'=8] {'gz','gy'}, dimensions={0} | all-to-all | bytes 1179648 | tf_op jit(solution)/shard_map/all_to_all | solution.py:234
  29.6 0.0 copy-done.5
  29.6 0.0 copy-done.6
  29.6 2.2 %shard_map.56 = f32[1152,128]{1,0:T(8,128)S(1)} custom-call(f32[1152,128]{1,0:T(8,128)S(1)} %bitcast.4, bf16[384,384]{1,0:T(8,128)(2,1)S(1)} %copy-done.6, bf16[384,384]{1,0:T(8,128)(2,1)S(1)} %copy-done.5), custom_call_target="tpu_custom_call" | custom-call | tf_op jit(solution)/shard_map/pallas_call | solution.py:223
  31.7 0.0 copy-start.1
  31.8 0.0 copy-start.3
  31.8 18.7 %all_to_all.11 = f32[128,1,1152]{2,1,0:T(1,128)S(1)} all-to-all(f32[128,1,1152]{2,1,0:T(1,128)S(1)} %bitcast.5), channel_id=1, replica_groups=mesh['gz'=16,'gy'=8] {'gz','gy'}, dimensions={0} | all-to-all | bytes 1179648 | tf_op jit(solution)/shard_map/all_to_all | solution.py:234
  50.5 0.0 copy-done.1
  50.5 0.0 copy-done.3
  50.5 1.8 %shard_map.57 = f32[8,15488]{1,0:T(8,128)} custom-call(f32[1152,128]{1,0:T(8,128)S(1)} %bitcast.6, bf16[384,384]{1,0:T(8,128)(2,1)S(1)} %copy-done.3, bf16[384,384]{1,0:T(8,128)(2,1)S(1)} %copy-done.1), custom_call_target="tpu_custom_call" | custom-call | tf_op jit(solution)/shard_map/pallas_call | solution.py:223
Async XLA Ops:
  0.0 1.0 %copy-start = (bf16[384,384]{1,0:T(8,128)(2,1)S(1)}, bf16[384,384]{1,0:T(8,128)(2,1)}, u32[]{:S(2)}) copy-start(bf16[384,384]{1,0:T(8,128)(2,1)} %constant.9.clone.low_ref) | copy-start | bytes 884740
  1.0 1.0 %copy-start.2 = (bf16[384,384]{1,0:T(8,128)(2,1)S(1)}, bf16[384,384]{1,0:T(8,128)(2,1)}, u32[]{:S(2)}) copy-start(bf16[384,384]{1,0:T(8,128)(2,1)} %constant.8.clone.high_ref) | copy-start | bytes 884740
  1.9 1.0 %copy-start.4 = (f32[8,15488]{1,0:T(8,128)S(1)}, f32[8,15488]{1,0:T(8,128)}, u32[]{:S(2)}) copy-start(f32[8,15488]{1,0:T(8,128)} %x_ref.1) | copy-start | bytes 1486852
  3.9 25.6 %copy-start.5 = (bf16[384,384]{1,0:T(8,128)(2,1)S(1)}, bf16[384,384]{1,0:T(8,128)(2,1)}, u32[]{:S(2)}) copy-start(bf16[384,384]{1,0:T(8,128)(2,1)} %constant.11.clone.low_ref) | copy-start | bytes 884740
  4.0 25.6 %copy-start.6 = (bf16[384,384]{1,0:T(8,128)(2,1)S(1)}, bf16[384,384]{1,0:T(8,128)(2,1)}, u32[]{:S(2)}) copy-start(bf16[384,384]{1,0:T(8,128)(2,1)} %constant.10.clone.high_ref) | copy-start | bytes 884740
  31.7 18.7 %copy-start.1 = (bf16[384,384]{1,0:T(8,128)(2,1)S(1)}, bf16[384,384]{1,0:T(8,128)(2,1)}, u32[]{:S(2)}) copy-start(bf16[384,384]{1,0:T(8,128)(2,1)} %constant.9.clone.low_ref) | copy-start | bytes 884740
  31.8 18.7 %copy-start.3 = (bf16[384,384]{1,0:T(8,128)(2,1)S(1)}, bf16[384,384]{1,0:T(8,128)(2,1)}, u32[]{:S(2)}) copy-start(bf16[384,384]{1,0:T(8,128)(2,1)} %constant.8.clone.high_ref) | copy-start | bytes 884740

commit v3 on v2

v3 whole, which is shorter than its diff:
```python
import math

import jax
import jax.numpy as jnp
import numpy as np
from jax import lax
from jax.experimental import pallas as pl
from jax.experimental.pallas import tpu as pltpu
from jax.sharding import PartitionSpec as P

NX = 352
NY = 352
SCREEN = 128
TWO_PI = 2.0 * math.pi

PAD = 384
LANES = 128
TILES = PAD // LANES
HALF = NX // 2
SLOT = PAD // 2
PAIR = 2 * LANES
GZ = 16
GY = 8
PLANES = 8
ROWS = NY // GY
CHUNK = PAD // GY
GROUP = 8 * HALF
OWN = 3
PEERS = GZ * GY
SEND = PEERS * OWN * TILES
BELONG = OWN * TILES

F32 = jnp.float32
BF16 = jnp.bfloat16


def component(parity, row):
    return 2 * ((row + 1 - parity) >> 1) + parity


def half_basis(length):
    half = length // 2
    index = np.arange(half)
    basis = np.zeros((2, half, half))
    for parity in range(2):
        for row in range(half):
            m = component(parity, row)
            angle = 2.0 * np.pi * ((m * index) % length) / length
            cosine = row == 0 or (row + parity) % 2 == 1 or m == half
            if parity == 1:
                cosine = row % 2 == 0
            weight = 1.0 if m in (0, half) else 2.0
            basis[parity, row] = (np.cos(angle) if cosine else np.sin(angle)) * np.sqrt(weight / length)
    return basis


def halves(table):
    single = table.astype(np.float32)
    high = single.astype(jnp.bfloat16)
    low = (single - high.astype(np.float32)).astype(jnp.bfloat16)
    return np.stack([high, low])


def x_table():
    table = np.zeros((2, SLOT, PAIR))
    table[:, :HALF, :HALF] = half_basis(NX)
    return halves(table)


def y_table():
    block = np.zeros((2, SLOT, GY // 2, CHUNK))
    block[:, :HALF, :, :ROWS] = half_basis(NY).reshape(2, HALF, GY // 2, ROWS)
    block = block.reshape(2, SLOT, SLOT)
    table = np.zeros((2, PAIR, PAIR))
    table[0, :SLOT, :SLOT] = block[0]
    table[1, PAIR - SLOT :, PAIR - SLOT :] = block[1]
    return halves(table)


def split(value):
    high = value.astype(BF16)
    return high, (value - high.astype(F32)).astype(BF16)


def product(left, right, dims):
    def dot(a, b):
        return lax.dot_general(a, b, (dims, ((), ())), preferred_element_type=F32)

    return dot(left[0], right[0]) + (dot(left[0], right[1]) + dot(left[1], right[0]))


def lane_tile(j):
    return slice(j * LANES, (j + 1) * LANES)


def table_of(table_ref, parity):
    return table_ref[0, parity], table_ref[1, parity]


def half_row(ref, offset):
    shift = offset % LANES
    width = -(-(shift + HALF) // LANES) * LANES
    value = ref[:, pl.ds(offset - shift, width)]
    if shift:
        value = pltpu.roll(value, width - shift, 1)
    return value[:, :PAIR]


def forward_x(x_ref, table_ref, out_ref, field_ref, flat_ref, local_ref, x_sems, table_sem):
    loads = []
    for n in range(NX * ROWS // GROUP):
        part = pl.ds(n * GROUP, GROUP)
        loads.append(pltpu.make_async_copy(x_ref.at[:, part], flat_ref.at[:, part], x_sems.at[n]))
    table_load = pltpu.make_async_copy(table_ref, local_ref, table_sem)
    for load in loads:
        load.start()
    table_load.start()
    for y in range(ROWS, CHUNK):
        for j in range(4):
            field_ref[j, pl.ds(y, PLANES, stride=CHUNK), :] = jnp.zeros((PLANES, LANES), F32)
    for n, load in enumerate(loads):
        load.wait()
        for y in range(n * GROUP // NX, (n + 1) * GROUP // NX):
            one = half_row(flat_ref, y * NX)
            two = half_row(flat_ref, y * NX + HALF)
            for parity, value in enumerate((one + two, one - two)):
                for j in range(2):
                    field_ref[2 * parity + j, pl.ds(y, PLANES, stride=CHUNK), :] = value[:, lane_tile(j)]
    table_load.wait()
    for parity in range(2):
        field = jnp.concatenate([field_ref[2 * parity + j] for j in range(2)], axis=1)
        result = product(table_of(local_ref, parity), split(field), ((1,), (1,)))
        for j in range(TILES):
            out_ref[pl.ds(parity * SLOT * TILES + j, SLOT, stride=TILES), :] = result[:, lane_tile(j)]


def chunk_pick(parts, lane):
    out = []
    for j in range(TILES):
        first = j * LANES // CHUNK
        last = ((j + 1) * LANES - 1) // CHUNK
        value = parts[last][j]
        for c in range(last - 1, first - 1, -1):
            value = jnp.where(lane < (c + 1) * CHUNK - j * LANES, parts[c][j], value)
        out.append(value)
    return out


def swap_chunks(arrays, lane):
    turned = []
    for d in range(GY):
        picked = chunk_pick([arrays[(c + d) % GY] for c in range(GY)], lane)
        whole = jnp.concatenate(picked, axis=1)
        if d:
            whole = pltpu.roll(whole, CHUNK * d, 1)
        turned.append([whole[:, lane_tile(j)] for j in range(TILES)])
    return [chunk_pick([turned[(c - b) % GY] for c in range(GY)], lane) for b in range(GY)]


def butterfly(arrays):
    pairs = [list(zip(arrays[g], arrays[g + GY // 2])) for g in range(GY // 2)]
    return [[a + b for a, b in p] for p in pairs] + [[a - b for a, b in p] for p in pairs]


def both_parities(value_ref, table_ref, dims, out_ref):
    even = product(split(value_ref[:, :PAIR]), table_of(table_ref, 0), dims)
    odd = product(split(value_ref[:, PAD - PAIR :]), table_of(table_ref, 1), dims)
    out_ref[:, lane_tile(0)] = even[:, :LANES]
    out_ref[:, lane_tile(1)] = even[:, LANES:] + odd[:, :LANES]
    out_ref[:, lane_tile(2)] = odd[:, LANES:]


def wavenumber(index, length):
    parity = (index >= SLOT).astype(jnp.int32)
    row = jnp.minimum(index - SLOT * parity, HALF - 1)
    return component(parity, row).astype(F32) * (TWO_PI / length)


def kappa_tile(own, j):
    device = lax.axis_index("gz") * GY + lax.axis_index("gy")
    index_x = jnp.full((GZ, LANES), device * OWN + own, jnp.int32)
    index_y = lax.broadcasted_iota(jnp.int32, (GZ, LANES), 1) + j * LANES
    wave_x = wavenumber(index_x, NX)
    wave_y = wavenumber(index_y, NY)
    return jnp.sqrt(1.0 / (SCREEN * SCREEN) + wave_x * wave_x + wave_y * wave_y)


def message_row(half, g, own, j):
    return pl.ds((half * 8 * GY + g) * BELONG + own * TILES + j, 8, stride=GY * BELONG)


def middle(in_ref, table_ref, out_ref, work_ref, phi_ref):
    lane = lax.broadcasted_iota(jnp.int32, (8, LANES), 1)
    block = OWN * GZ
    for tile in range(block // 8):
        own, half = divmod(tile, GZ // 8)
        arrays = [[in_ref[message_row(half, g, own, j), :] for j in range(TILES)] for g in range(GY)]
        for z, parts in enumerate(swap_chunks(butterfly(arrays), lane)):
            for j in range(TILES):
                work_ref[pl.ds(z * block + tile * 8, 8), lane_tile(j)] = parts[j]
    both_parities(work_ref, table_ref, ((1,), (1,)), phi_ref)

    gz = lax.broadcasted_iota(jnp.int32, (GZ, LANES), 0)
    for own in range(OWN):
        for j in range(TILES):
            kappa = kappa_tile(own, j)
            decay = jnp.exp(-kappa)
            scale = 0.5 / kappa
            hat = [phi_ref[pl.ds(z * block + own * GZ, GZ), lane_tile(j)] for z in range(PLANES)]
            up = [hat[0]]
            for z in range(1, PLANES):
                up.append(decay * up[-1] + hat[z])
            down = [jnp.zeros((GZ, LANES), F32)]
            for z in range(PLANES - 1, 0, -1):
                down.append(decay * (down[-1] + hat[z]))
            down = down[::-1]
            over = up[-1]
            under = decay * (down[0] + hat[0])
            power = decay * decay
            power = power * power
            power = power * power
            step = 1
            while step < GZ:
                over = over + jnp.where(gz >= step, power * pltpu.roll(over, step, 0), 0.0)
                under = under + jnp.where(gz < GZ - step, power * pltpu.roll(under, GZ - step, 0), 0.0)
                power = power * power
                step *= 2
            over = jnp.where(gz >= 1, pltpu.roll(over, 1, 0), 0.0)
            under = jnp.where(gz < GZ - 1, pltpu.roll(under, GZ - 1, 0), 0.0)
            for z in range(PLANES):
                over = decay * over
                up[z] = up[z] + over
            for z in range(PLANES - 1, -1, -1):
                down[z] = down[z] + under
                under = decay * under
            for z in range(PLANES):
                phi_ref[pl.ds(z * block + own * GZ, GZ), lane_tile(j)] = (up[z] + down[z]) * scale

    both_parities(phi_ref, table_ref, ((1,), (0,)), work_ref)
    for tile in range(block // 8):
        own, half = divmod(tile, GZ // 8)
        arrays = [
            [work_ref[pl.ds(z * block + tile * 8, 8), lane_tile(j)] for j in range(TILES)] for z in range(PLANES)
        ]
        for g, parts in enumerate(butterfly(swap_chunks(arrays, lane))):
            for j in range(TILES):
                out_ref[message_row(half, g, own, j), :] = parts[j]


def backward_x(in_ref, table_ref, out_ref, field_ref, flat_ref, sems):
    parts = []
    for parity in range(2):
        rows = [pl.ds(parity * SLOT * TILES + j, SLOT, stride=TILES) for j in range(TILES)]
        value = jnp.concatenate([in_ref[row, :] for row in rows], axis=1)
        parts.append(product(split(jnp.transpose(value)), table_of(table_ref, parity), ((1,), (0,))))
    for side, value in enumerate((parts[0] + parts[1], parts[0] - parts[1])):
        for j in range(2):
            field_ref[2 * side + j] = value[:, lane_tile(j)]
    stores = []
    carry = None
    for piece in range(2 * ROWS):
        y, side = divmod(piece, 2)
        offset = piece * HALF
        shift = offset % LANES
        end = shift + HALF
        tiles = [field_ref[2 * side + j, pl.ds(y, PLANES, stride=CHUNK), :] for j in range(2)]
        if end > PAIR:
            tiles.append(jnp.zeros((PLANES, LANES), F32))
        if shift:
            value = pltpu.roll(jnp.concatenate(tiles, axis=1), shift, 1)
            tiles = [value[:, lane_tile(j)] for j in range(len(tiles))]
        if carry is not None:
            tiles[0] = tiles[0] + carry
        full = end // LANES
        carry = tiles[full] if end % LANES else None
        for j in range(full):
            flat_ref[:, pl.ds(offset - shift + j * LANES, LANES)] = tiles[j]
        if (offset + HALF) % GROUP == 0:
            n = offset // GROUP
            part = pl.ds(n * GROUP, GROUP)
            stores.append(pltpu.make_async_copy(flat_ref.at[:, part], out_ref.at[:, part], sems.at[n]))
            stores[-1].start()
    for store in stores:
        store.wait()


def exchange(buffer):
    whole = buffer.reshape(PEERS, 1, BELONG * LANES)
    whole = lax.all_to_all(whole, ("gz", "gy"), 0, 0, tiled=True)
    return whole.reshape(SEND, LANES)


def on_device(density):
    table_x = jnp.asarray(x_table())
    table_y = jnp.asarray(y_table())
    vmem = pl.BlockSpec(memory_space=pltpu.VMEM)
    hbm = pl.BlockSpec(memory_space=pl.ANY)
    field = pltpu.VMEM((4, PAD, LANES), F32)
    flat = pltpu.VMEM(density.shape, F32)
    square = pltpu.VMEM((PAD, PAD), F32)
    message = pltpu.VMEM((SEND, LANES), F32)
    groups = pltpu.SemaphoreType.DMA((NX * ROWS // GROUP,))

    def here(value):
        return pltpu.with_memory_space_constraint(value, pltpu.VMEM)

    sent = pl.pallas_call(
        forward_x,
        out_shape=message,
        in_specs=[hbm, hbm],
        out_specs=vmem,
        scratch_shapes=[
            field,
            flat,
            pltpu.VMEM(table_x.shape, BF16),
            groups,
            pltpu.SemaphoreType.DMA,
        ],
    )(density, table_x)
    back = pl.pallas_call(
        middle,
        out_shape=message,
        in_specs=[vmem, vmem],
        out_specs=vmem,
        scratch_shapes=[square, square],
    )(here(exchange(sent)), here(table_y))
    return pl.pallas_call(
        backward_x,
        out_shape=jax.ShapeDtypeStruct(density.shape, F32),
        in_specs=[vmem, vmem],
        out_specs=hbm,
        scratch_shapes=[field, flat, groups],
    )(here(exchange(back)), here(table_x))


def solution(mesh):
    return jax.shard_map(
        on_device,
        mesh=mesh,
        in_specs=(P("gz", "gy"),),
        out_specs=P("gz", "gy"),
        check_vma=False,
    )
```

time: 52.5 us -> 50.2 us (0.956)
  local copies, waits for them, and re-layouts: 2.98 us -> 0.01 us
  Pallas kernels: 4.91 us -> 5.68 us
    unnamed x14 -> x4, local copies, waits for them, and re-layouts: 2.98 us -> 0.01 us
    pallas_call x3, Pallas kernels: 4.91 us -> 5.68 us  [the longest x1 2.55 us: on_device(): pl.pallas_call(forward_x, out_shape=message, in_specs=[hbm, hbm], out_spe...]
where the time goes in v3:
time: 50.2 us; the launch traced here: 50 us
  blocking collectives  44.3 us (88%)
  Pallas kernels  5.68 us (11%)
    all_to_all x2, blocking collectives, exchange(): whole = lax.all_to_all(whole, ('gz', 'gy'), 0, 0, tiled=True)  44.3 us
    pallas_call x1, Pallas kernels, on_device(): pl.pallas_call(forward_x, out_shape=message, in_specs=[hbm, hbm], out_spe...  2.55 us
    pallas_call x1, Pallas kernels, on_device(): pl.pallas_call(backward_x, out_shape=jax.ShapeDtypeStruct(density.shape,...  1.62 us
    pallas_call x1, Pallas kernels, on_device(): pl.pallas_call(middle, out_shape=message, in_specs=[vmem, vmem], out_spec...  1.5 us

profile of v3, /device:TPU:1, one launch (start us, length us, event | category | flops | bytes accessed | tf_op | source)
XLA Modules:
  0.0 50.0 jit_solution(7669682739170219662)
XLA Ops:
  0.0 2.5 %shard_map.37 = f32[1152,128]{1,0:T(8,128)S(1)} custom-call(f32[8,15488]{1,0:T(8,128)} %x_ref.1, bf16[2,2,192,256]{3,2,1,0:T(8,128)(2,1)} %constant.4.clone.table_ref), custom_call_target="tpu_custom_call" | custom-call | tf_op jit(solution)/shard_map/pallas_call | solution.py:307
  2.6 0.0 copy-start.1
  2.6 25.6 %all_to_all.10 = f32[128,1,1152]{2,1,0:T(1,128)S(1)} all-to-all(f32[128,1,1152]{2,1,0:T(1,128)S(1)} %bitcast.7), channel_id=1, replica_groups=mesh['gz'=16,'gy'=8] {'gz','gy'}, dimensions={0} | all-to-all | bytes 1179648 | tf_op jit(solution)/shard_map/all_to_all | solution.py:289
  28.2 0.0 copy-done.1
  28.2 1.5 %shard_map.38 = f32[1152,128]{1,0:T(8,128)S(1)} custom-call(f32[1152,128]{1,0:T(8,128)S(1)} %bitcast.4, bf16[2,2,256,256]{3,2,1,0:T(8,128)(2,1)S(1)} %copy-done.1), custom_call_target="tpu_custom_call" | custom-call | tf_op jit(solution)/shard_map/pallas_call | solution.py:320
  29.7 0.0 copy-start
  29.7 18.7 %all_to_all.11 = f32[128,1,1152]{2,1,0:T(1,128)S(1)} all-to-all(f32[128,1,1152]{2,1,0:T(1,128)S(1)} %bitcast.5), channel_id=1, replica_groups=mesh['gz'=16,'gy'=8] {'gz','gy'}, dimensions={0} | all-to-all | bytes 1179648 | tf_op jit(solution)/shard_map/all_to_all | solution.py:289
  48.4 0.0 copy-done
  48.4 1.6 %shard_map.39 = f32[8,15488]{1,0:T(8,128)} custom-call(f32[1152,128]{1,0:T(8,128)S(1)} %bitcast.6, bf16[2,2,192,256]{3,2,1,0:T(8,128)(2,1)S(1)} %copy-done), custom_call_target="tpu_custom_call" | custom-call | tf_op jit(solution)/shard_map/pallas_call | solution.py:327
Async XLA Ops:
  2.6 25.6 %copy-start.1 = (bf16[2,2,256,256]{3,2,1,0:T(8,128)(2,1)S(1)}, bf16[2,2,256,256]{3,2,1,0:T(8,128)(2,1)}, u32[]{:S(2)}) copy-start(bf16[2,2,256,256]{3,2,1,0:T(8,128)(2,1)} %constant.5.clone.table_ref) | copy-start | bytes 1572868
  29.7 18.7 %copy-start = (bf16[2,2,192,256]{3,2,1,0:T(8,128)(2,1)S(1)}, bf16[2,2,192,256]{3,2,1,0:T(8,128)(2,1)}, u32[]{:S(2)}) copy-start(bf16[2,2,192,256]{3,2,1,0:T(8,128)(2,1)} %constant.4.clone.table_ref) | copy-start | bytes 1179652

commit v4 on v3

--- a/solution.py
+++ b/solution.py
@@ -24,7 +24,8 @@
 PLANES = 8
 ROWS = NY // GY
 CHUNK = PAD // GY
-GROUP = 8 * HALF
+PITCH = PLANES + 1
+PARTS = (0, 24, ROWS)
 OWN = 3
 PEERS = GZ * GY
 SEND = PEERS * OWN * TILES
@@ -97,19 +98,27 @@
     return table_ref[0, parity], table_ref[1, parity]
 
 
-def half_row(ref, offset):
+def shift_lanes(tiles, amount, lane):
+    count = len(tiles)
+    whole, part = divmod(amount % (count * LANES), LANES)
+    if part:
+        turned = [pltpu.roll(t, part, 1) for t in tiles]
+        tiles = [jnp.where(lane < part, turned[j - 1], turned[j]) for j in range(count)]
+    return [tiles[(j - whole) % count] for j in range(count)]
+
+
+def half_row(ref, offset, lane):
     shift = offset % LANES
-    width = -(-(shift + HALF) // LANES) * LANES
-    value = ref[:, pl.ds(offset - shift, width)]
-    if shift:
-        value = pltpu.roll(value, width - shift, 1)
-    return value[:, :PAIR]
+    count = -(-(shift + HALF) // LANES)
+    tiles = [ref[:, pl.ds(offset - shift + j * LANES, LANES)] for j in range(count)]
+    return shift_lanes(tiles, -shift, lane)[:2]
 
 
 def forward_x(x_ref, table_ref, out_ref, field_ref, flat_ref, local_ref, x_sems, table_sem):
+    lane = lax.broadcasted_iota(jnp.int32, (PLANES, LANES), 1)
     loads = []
-    for n in range(NX * ROWS // GROUP):
-        part = pl.ds(n * GROUP, GROUP)
+    for n, (first, last) in enumerate(zip(PARTS, PARTS[1:])):
+        part = pl.ds(first * NX, (last - first) * NX)
         loads.append(pltpu.make_async_copy(x_ref.at[:, part], flat_ref.at[:, part], x_sems.at[n]))
     table_load = pltpu.make_async_copy(table_ref, local_ref, table_sem)
     for load in loads:
@@ -117,18 +126,26 @@
     table_load.start()
     for y in range(ROWS, CHUNK):
         for j in range(4):
-            field_ref[j, pl.ds(y, PLANES, stride=CHUNK), :] = jnp.zeros((PLANES, LANES), F32)
-    for n, load in enumerate(loads):
+            field_ref[j, pl.ds(y * PITCH, PLANES), :] = jnp.zeros((PLANES, LANES), F32)
+    for load, first, last in zip(loads, PARTS, PARTS[1:]):
         load.wait()
-        for y in range(n * GROUP // NX, (n + 1) * GROUP // NX):
-            one = half_row(flat_ref, y * NX)
-            two = half_row(flat_ref, y * NX + HALF)
-            for parity, value in enumerate((one + two, one - two)):
-                for j in range(2):
-                    field_ref[2 * parity + j, pl.ds(y, PLANES, stride=CHUNK), :] = value[:, lane_tile(j)]
+        for y in range(first, last):
+            one = half_row(flat_ref, y * NX, lane)
+            two = half_row(flat_ref, y * NX + HALF, lane)
+            for j in range(2):
+                field_ref[j, pl.ds(y * PITCH, PLANES), :] = one[j] + two[j]
+                field_ref[2 + j, pl.ds(y * PITCH, PLANES), :] = one[j] - two[j]
     table_load.wait()
     for parity in range(2):
-        field = jnp.concatenate([field_ref[2 * parity + j] for j in range(2)], axis=1)
+        columns = []
+        for j in range(2):
+            rows = [
+                field_ref[2 * parity + j, pl.ds(z + y * PITCH, 8, stride=PITCH), :]
+                for z in range(PLANES)
+                for y in range(0, CHUNK, 8)
+            ]
+            columns.append(jnp.concatenate(rows, axis=0))
+        field = jnp.concatenate(columns, axis=1)
         result = product(table_of(local_ref, parity), split(field), ((1,), (1,)))
         for j in range(TILES):
             out_ref[pl.ds(parity * SLOT * TILES + j, SLOT, stride=TILES), :] = result[:, lane_tile(j)]
@@ -150,10 +167,7 @@
     turned = []
     for d in range(GY):
         picked = chunk_pick([arrays[(c + d) % GY] for c in range(GY)], lane)
-        whole = jnp.concatenate(picked, axis=1)
-        if d:
-            whole = pltpu.roll(whole, CHUNK * d, 1)
-        turned.append([whole[:, lane_tile(j)] for j in range(TILES)])
+        turned.append(shift_lanes(picked, CHUNK * d, lane))
     return [chunk_pick([turned[(c - b) % GY] for c in range(GY)], lane) for b in range(GY)]
 
 
@@ -255,7 +269,11 @@
         parts.append(product(split(jnp.transpose(value)), table_of(table_ref, parity), ((1,), (0,))))
     for side, value in enumerate((parts[0] + parts[1], parts[0] - parts[1])):
         for j in range(2):
-            field_ref[2 * side + j] = value[:, lane_tile(j)]
+            for z in range(PLANES):
+                for y in range(0, CHUNK, 8):
+                    rows = pl.ds(z + y * PITCH, 8, stride=PITCH)
+                    field_ref[2 * side + j, rows, :] = value[z * CHUNK + y : z * CHUNK + y + 8, lane_tile(j)]
+    lane = lax.broadcasted_iota(jnp.int32, (PLANES, LANES), 1)
     stores = []
     carry = None
     for piece in range(2 * ROWS):
@@ -263,21 +281,19 @@
         offset = piece * HALF
         shift = offset % LANES
         end = shift + HALF
-        tiles = [field_ref[2 * side + j, pl.ds(y, PLANES, stride=CHUNK), :] for j in range(2)]
+        tiles = [field_ref[2 * side + j, pl.ds(y * PITCH, PLANES), :] for j in range(2)]
         if end > PAIR:
             tiles.append(jnp.zeros((PLANES, LANES), F32))
-        if shift:
-            value = pltpu.roll(jnp.concatenate(tiles, axis=1), shift, 1)
-            tiles = [value[:, lane_tile(j)] for j in range(len(tiles))]
+        tiles = shift_lanes(tiles, shift, lane)
         if carry is not None:
             tiles[0] = tiles[0] + carry
         full = end // LANES
         carry = tiles[full] if end % LANES else None
         for j in range(full):
             flat_ref[:, pl.ds(offset - shift + j * LANES, LANES)] = tiles[j]
-        if (offset + HALF) % GROUP == 0:
-            n = offset // GROUP
-            part = pl.ds(n * GROUP, GROUP)
+        if side == 1 and y + 1 in PARTS:
+            n = PARTS.index(y + 1) - 1
+            part = pl.ds(PARTS[n] * NX, (y + 1 - PARTS[n]) * NX)
             stores.append(pltpu.make_async_copy(flat_ref.at[:, part], out_ref.at[:, part], sems.at[n]))
             stores[-1].start()
     for store in stores:
@@ -295,11 +311,11 @@
     table_y = jnp.asarray(y_table())
     vmem = pl.BlockSpec(memory_space=pltpu.VMEM)
     hbm = pl.BlockSpec(memory_space=pl.ANY)
-    field = pltpu.VMEM((4, PAD, LANES), F32)
+    field = pltpu.VMEM((4, CHUNK * PITCH, LANES), F32)
     flat = pltpu.VMEM(density.shape, F32)
     square = pltpu.VMEM((PAD, PAD), F32)
     message = pltpu.VMEM((SEND, LANES), F32)
-    groups = pltpu.SemaphoreType.DMA((NX * ROWS // GROUP,))
+    groups = pltpu.SemaphoreType.DMA((len(PARTS) - 1,))
 
     def here(value):
         return pltpu.with_memory_space_constraint(value, pltpu.VMEM)

time: 50.2 us -> 49.5 us (0.986)
  Pallas kernels: 5.68 us -> 4.94 us
    pallas_call x1, Pallas kernels: 2.55 us -> 1.86 us  [on_device(): pl.pallas_call(forward_x, out_shape=message, in_specs=[hbm, hbm], out_spe...]
where the time goes in v4:
time: 49.5 us; the launch traced here: 49.3 us
  blocking collectives  44.3 us (89%)
  Pallas kernels  4.94 us (10%)
    all_to_all x2, blocking collectives, exchange(): whole = lax.all_to_all(whole, ('gz', 'gy'), 0, 0, tiled=True)  44.3 us
    pallas_call x1, Pallas kernels, on_device(): pl.pallas_call(forward_x, out_shape=message, in_specs=[hbm, hbm], out_spe...  1.86 us
    pallas_call x1, Pallas kernels, on_device(): pl.pallas_call(backward_x, out_shape=jax.ShapeDtypeStruct(density.shape,...  1.6 us
    pallas_call x1, Pallas kernels, on_device(): pl.pallas_call(middle, out_shape=message, in_specs=[vmem, vmem], out_spec...  1.48 us

profile of v4, /device:TPU:1, one launch (start us, length us, event | category | flops | bytes accessed | tf_op | source)
XLA Modules:
  0.0 49.3 jit_solution(3865400943851779760)
XLA Ops:
  0.0 1.9 %shard_map.37 = f32[1152,128]{1,0:T(8,128)S(1)} custom-call(f32[8,15488]{1,0:T(8,128)} %x_ref.1, bf16[2,2,192,256]{3,2,1,0:T(8,128)(2,1)} %constant.4.clone.table_ref), custom_call_target="tpu_custom_call" | custom-call | tf_op jit(solution)/shard_map/pallas_call | solution.py:323
  1.9 0.0 copy-start.1
  1.9 25.6 %all_to_all.10 = f32[128,1,1152]{2,1,0:T(1,128)S(1)} all-to-all(f32[128,1,1152]{2,1,0:T(1,128)S(1)} %bitcast.7), channel_id=1, replica_groups=mesh['gz'=16,'gy'=8] {'gz','gy'}, dimensions={0} | all-to-all | bytes 1179648 | tf_op jit(solution)/shard_map/all_to_all | solution.py:305
  27.5 0.0 copy-done.1
  27.5 1.5 %shard_map.38 = f32[1152,128]{1,0:T(8,128)S(1)} custom-call(f32[1152,128]{1,0:T(8,128)S(1)} %bitcast.4, bf16[2,2,256,256]{3,2,1,0:T(8,128)(2,1)S(1)} %copy-done.1), custom_call_target="tpu_custom_call" | custom-call | tf_op jit(solution)/shard_map/pallas_call | solution.py:336
  29.0 0.0 copy-start
  29.0 18.7 %all_to_all.11 = f32[128,1,1152]{2,1,0:T(1,128)S(1)} all-to-all(f32[128,1,1152]{2,1,0:T(1,128)S(1)} %bitcast.5), channel_id=1, replica_groups=mesh['gz'=16,'gy'=8] {'gz','gy'}, dimensions={0} | all-to-all | bytes 1179648 | tf_op jit(solution)/shard_map/all_to_all | solution.py:305
  47.7 0.0 copy-done
  47.7 1.6 %shard_map.39 = f32[8,15488]{1,0:T(8,128)} custom-call(f32[1152,128]{1,0:T(8,128)S(1)} %bitcast.6, bf16[2,2,192,256]{3,2,1,0:T(8,128)(2,1)S(1)} %copy-done), custom_call_target="tpu_custom_call" | custom-call | tf_op jit(solution)/shard_map/pallas_call | solution.py:343
Async XLA Ops:
  1.9 25.6 %copy-start.1 = (bf16[2,2,256,256]{3,2,1,0:T(8,128)(2,1)S(1)}, bf16[2,2,256,256]{3,2,1,0:T(8,128)(2,1)}, u32[]{:S(2)}) copy-start(bf16[2,2,256,256]{3,2,1,0:T(8,128)(2,1)} %constant.5.clone.table_ref) | copy-start | bytes 1572868
  29.0 18.7 %copy-start = (bf16[2,2,192,256]{3,2,1,0:T(8,128)(2,1)S(1)}, bf16[2,2,192,256]{3,2,1,0:T(8,128)(2,1)}, u32[]{:S(2)}) copy-start(bf16[2,2,192,256]{3,2,1,0:T(8,128)(2,1)} %constant.4.clone.table_ref) | copy-start | bytes 1179652

commit v5 on v4

--- a/solution.py
+++ b/solution.py
@@ -6,6 +6,7 @@
 from jax import lax
 from jax.experimental import pallas as pl
 from jax.experimental.pallas import tpu as pltpu
+from jax.sharding import Mesh
 from jax.sharding import PartitionSpec as P
 
 NX = 352
@@ -20,16 +21,19 @@
 SLOT = PAD // 2
 PAIR = 2 * LANES
 GZ = 16
-GY = 8
+GX = 4
+CORES = 2
+GY = GX * CORES
 PLANES = 8
 ROWS = NY // GY
 CHUNK = PAD // GY
 PITCH = PLANES + 1
 PARTS = (0, 24, ROWS)
 OWN = 3
-PEERS = GZ * GY
-SEND = PEERS * OWN * TILES
-BELONG = OWN * TILES
+CHIPS = GZ * GX
+SWAP = SLOT * TILES
+STRIDE = CORES * TILES
+SEND = SLOT * STRIDE
 
 F32 = jnp.float32
 BF16 = jnp.bfloat16
@@ -114,7 +118,29 @@
     return shift_lanes(tiles, -shift, lane)[:2]
 
 
-def forward_x(x_ref, table_ref, out_ref, field_ref, flat_ref, local_ref, x_sems, table_sem):
+def sign_of(parity):
+    return (1 - 2 * parity).astype(F32)
+
+
+def part_of_field(field_ref, parity):
+    columns = []
+    for j in range(2):
+        rows = []
+        for z in range(PLANES):
+            for y in range(0, CHUNK, 8):
+                at = pl.ds(z + y * PITCH, 8, stride=PITCH)
+                rows.append(field_ref[j, at, :] + sign_of(parity) * field_ref[2 + j, at, :])
+        columns.append(jnp.concatenate(rows, axis=0))
+    return jnp.concatenate(columns, axis=1)
+
+
+def components(field_ref, table_ref, parity, out_ref):
+    result = product(table_of(table_ref, parity), split(part_of_field(field_ref, parity)), ((1,), (1,)))
+    for j in range(TILES):
+        out_ref[pl.ds(j, SLOT, stride=TILES), :] = result[:, lane_tile(j)]
+
+
+def forward_other(x_ref, table_ref, out_ref, field_ref, local_ref, flat_ref, x_sems, table_sem):
     lane = lax.broadcasted_iota(jnp.int32, (PLANES, LANES), 1)
     loads = []
     for n, (first, last) in enumerate(zip(PARTS, PARTS[1:])):
@@ -130,25 +156,29 @@
     for load, first, last in zip(loads, PARTS, PARTS[1:]):
         load.wait()
         for y in range(first, last):
-            one = half_row(flat_ref, y * NX, lane)
-            two = half_row(flat_ref, y * NX + HALF, lane)
-            for j in range(2):
-                field_ref[j, pl.ds(y * PITCH, PLANES), :] = one[j] + two[j]
-                field_ref[2 + j, pl.ds(y * PITCH, PLANES), :] = one[j] - two[j]
+            for side in range(2):
+                tiles = half_row(flat_ref, y * NX + side * HALF, lane)
+                for j in range(2):
+                    field_ref[2 * side + j, pl.ds(y * PITCH, PLANES), :] = tiles[j]
     table_load.wait()
-    for parity in range(2):
-        columns = []
-        for j in range(2):
-            rows = [
-                field_ref[2 * parity + j, pl.ds(z + y * PITCH, 8, stride=PITCH), :]
-                for z in range(PLANES)
-                for y in range(0, CHUNK, 8)
-            ]
-            columns.append(jnp.concatenate(rows, axis=0))
-        field = jnp.concatenate(columns, axis=1)
-        result = product(table_of(local_ref, parity), split(field), ((1,), (1,)))
+    components(field_ref, local_ref, 1 - lax.axis_index("core"), out_ref)
+
+
+def forward_own(field_ref, table_ref, out_ref):
+    components(field_ref, table_ref, lax.axis_index("core"), out_ref)
+
+
+def merge(own_ref, other_ref, out_ref):
+    core = lax.axis_index("core")
+    for part_ref, at in ((own_ref, core), (other_ref, 1 - core)):
         for j in range(TILES):
-            out_ref[pl.ds(parity * SLOT * TILES + j, SLOT, stride=TILES), :] = result[:, lane_tile(j)]
+            out_ref[pl.ds(at * TILES + j, SLOT, stride=STRIDE), :] = part_ref[pl.ds(j, SLOT, stride=TILES), :]
+
+
+def pick_other(in_ref, out_ref):
+    at = 1 - lax.axis_index("core")
+    for j in range(TILES):
+        out_ref[pl.ds(j, SLOT, stride=TILES), :] = in_ref[pl.ds(at * TILES + j, SLOT, stride=STRIDE), :]
 
 
 def chunk_pick(parts, lane):
@@ -191,8 +221,8 @@
 
 
 def kappa_tile(own, j):
-    device = lax.axis_index("gz") * GY + lax.axis_index("gy")
-    index_x = jnp.full((GZ, LANES), device * OWN + own, jnp.int32)
+    chip = lax.axis_index("gz") * GX + lax.axis_index("x")
+    index_x = jnp.full((GZ, LANES), lax.axis_index("core") * SLOT + chip * OWN + own, jnp.int32)
     index_y = lax.broadcasted_iota(jnp.int32, (GZ, LANES), 1) + j * LANES
     wave_x = wavenumber(index_x, NX)
     wave_y = wavenumber(index_y, NY)
@@ -200,7 +230,9 @@
 
 
 def message_row(half, g, own, j):
-    return pl.ds((half * 8 * GY + g) * BELONG + own * TILES + j, 8, stride=GY * BELONG)
+    x, core = divmod(g, CORES)
+    first = ((half * 8 * GX + x) * OWN + own) * STRIDE + core * TILES + j
+    return pl.ds(first, 8, stride=GX * OWN * STRIDE)
 
 
 def middle(in_ref, table_ref, out_ref, work_ref, phi_ref):
@@ -261,13 +293,24 @@
                 out_ref[message_row(half, g, own, j), :] = parts[j]
 
 
-def backward_x(in_ref, table_ref, out_ref, field_ref, flat_ref, sems):
-    parts = []
-    for parity in range(2):
-        rows = [pl.ds(parity * SLOT * TILES + j, SLOT, stride=TILES) for j in range(TILES)]
-        value = jnp.concatenate([in_ref[row, :] for row in rows], axis=1)
-        parts.append(product(split(jnp.transpose(value)), table_of(table_ref, parity), ((1,), (0,))))
-    for side, value in enumerate((parts[0] + parts[1], parts[0] - parts[1])):
+def contribution(value, table_ref, parity):
+    return product(split(jnp.transpose(value)), table_of(table_ref, parity), ((1,), (0,)))
+
+
+def backward_own(in_ref, table_ref, out_ref):
+    core = lax.axis_index("core")
+    rows = [pl.ds(core * TILES + j, SLOT, stride=STRIDE) for j in range(TILES)]
+    value = jnp.concatenate([in_ref[row, :] for row in rows], axis=1)
+    out_ref[...] = contribution(value, table_ref, core)
+
+
+def backward_other(in_ref, own_ref, table_ref, out_ref, field_ref, flat_ref, sems):
+    core = lax.axis_index("core")
+    rows = [pl.ds(j, SLOT, stride=TILES) for j in range(TILES)]
+    value = jnp.concatenate([in_ref[row, :] for row in rows], axis=1)
+    other = contribution(value, table_ref, 1 - core)
+    own = own_ref[...]
+    for side, value in enumerate((own + other, (own - other) * sign_of(core))):
         for j in range(2):
             for z in range(PLANES):
                 for y in range(0, CHUNK, 8):
@@ -301,9 +344,13 @@
 
 
 def exchange(buffer):
-    whole = buffer.reshape(PEERS, 1, BELONG * LANES)
-    whole = lax.all_to_all(whole, ("gz", "gy"), 0, 0, tiled=True)
+    whole = buffer.reshape(CHIPS, 1, SEND // CHIPS * LANES)
+    whole = lax.all_to_all(whole, ("gz", "x"), 0, 0, tiled=True)
     return whole.reshape(SEND, LANES)
+
+
+def swap_cores(buffer):
+    return lax.ppermute(buffer, "core", [(0, 1), (1, 0)])
 
 
 def on_device(density):
@@ -315,45 +362,55 @@
     flat = pltpu.VMEM(density.shape, F32)
     square = pltpu.VMEM((PAD, PAD), F32)
     message = pltpu.VMEM((SEND, LANES), F32)
-    groups = pltpu.SemaphoreType.DMA((len(PARTS) - 1,))
+    half = pltpu.VMEM((SWAP, LANES), F32)
+    copies = pltpu.SemaphoreType.DMA((len(PARTS) - 1,))
 
     def here(value):
         return pltpu.with_memory_space_constraint(value, pltpu.VMEM)
 
-    sent = pl.pallas_call(
-        forward_x,
-        out_shape=message,
+    def call(kernel, out_shape, *args):
+        return pl.pallas_call(
+            kernel, out_shape=out_shape, in_specs=[vmem] * len(args), out_specs=vmem
+        )(*(here(a) for a in args))
+
+    give, fields, local_x = pl.pallas_call(
+        forward_other,
+        out_shape=(half, field, pltpu.VMEM(table_x.shape, BF16)),
         in_specs=[hbm, hbm],
-        out_specs=vmem,
-        scratch_shapes=[
-            field,
-            flat,
-            pltpu.VMEM(table_x.shape, BF16),
-            groups,
-            pltpu.SemaphoreType.DMA,
-        ],
+        out_specs=(vmem, vmem, vmem),
+        scratch_shapes=[flat, copies, pltpu.SemaphoreType.DMA],
     )(density, table_x)
+    taken = swap_cores(give)
+    kept = call(forward_own, half, fields, local_x)
+    held = exchange(call(merge, message, kept, taken))
+
     back = pl.pallas_call(
         middle,
         out_shape=message,
         in_specs=[vmem, vmem],
         out_specs=vmem,
         scratch_shapes=[square, square],
-    )(here(exchange(sent)), here(table_y))
+    )(here(held), here(table_y))
+
+    held = exchange(back)
+    taken = swap_cores(call(pick_other, half, held))
+    kept = call(backward_own, pltpu.VMEM((PAD, PAIR), F32), held, table_x)
     return pl.pallas_call(
-        backward_x,
+        backward_other,
         out_shape=jax.ShapeDtypeStruct(density.shape, F32),
-        in_specs=[vmem, vmem],
+        in_specs=[vmem, vmem, vmem],
         out_specs=hbm,
-        scratch_shapes=[field, flat, groups],
-    )(here(exchange(back)), here(table_x))
+        scratch_shapes=[field, flat, copies],
+    )(here(taken), here(kept), here(table_x))
 
 
 def solution(mesh):
+    chips = Mesh(mesh.devices.reshape(GZ, GX, CORES), ("gz", "x", "core"))
+    spec = P("gz", ("x", "core"))
     return jax.shard_map(
         on_device,
-        mesh=mesh,
-        in_specs=(P("gz", "gy"),),
-        out_specs=P("gz", "gy"),
+        mesh=chips,
+        in_specs=(spec,),
+        out_specs=spec,
         check_vma=False,
     )

time: 49.5 us -> 52.4 us (1.059)
  starting transfers between devices: 0 us -> 4.64 us
  blocking collectives: 44.3 us -> 40.5 us
  waiting for transfers between devices: 0 us -> 1.68 us
    ppermute x0 -> x2, starting transfers between devices: none -> 4.64 us  [swap_cores(): return lax.ppermute(buffer, 'core', [(0, 1), (1, 0)])]
    all_to_all x2, blocking collectives: 44.3 us -> 40.5 us  [exchange(): whole = lax.all_to_all(whole, ('gz', 'x'), 0, 0, tiled=True)]
    ppermute x0 -> x2, waiting for transfers between devices: none -> 1.68 us  [swap_cores(): return lax.ppermute(buffer, 'core', [(0, 1), (1, 0)])]
    pallas_call x2 -> x6, Pallas kernels: 3.46 us -> 3.81 us  [the longest x1 1.68 us: on_device(): pl.pallas_call(forward_other, out_shape=(half, field, pltpu.VMEM(table_x....]
  transfers between devices with their start and end apart: 0 -> 2, of which waited for: 0 -> 2; matrix products, arithmetic and copies ran while one was open for 0% -> 0% of each run, Pallas kernels for 0% -> 1%
where the time goes in v5:
time: 52.4 us; the launch traced here: 52.2 us
  blocking collectives  40.5 us (77%)
  Pallas kernels  5.29 us (10%)
  starting transfers between devices  4.64 us (9%)
  waiting for transfers between devices  1.68 us (3%)
    all_to_all x2, blocking collectives, exchange(): whole = lax.all_to_all(whole, ('gz', 'x'), 0, 0, tiled=True)  40.5 us
    ppermute x2, starting transfers between devices, swap_cores(): return lax.ppermute(buffer, 'core', [(0, 1), (1, 0)])  4.64 us
    pallas_call x1, Pallas kernels, on_device(): pl.pallas_call(forward_other, out_shape=(half, field, pltpu.VMEM(table_x....  1.68 us
    ppermute x2, waiting for transfers between devices, swap_cores(): return lax.ppermute(buffer, 'core', [(0, 1), (1, 0)])  1.68 us
    pallas_call x1, Pallas kernels, on_device(): pl.pallas_call(middle, out_shape=message, in_specs=[vmem, vmem], out_spec...  1.48 us
    pallas_call x1, Pallas kernels, on_device(): pl.pallas_call(backward_other, out_shape=jax.ShapeDtypeStruct(density.sha...  1.32 us
  transfers between devices with their start and end apart: 2, of which 2 were waited for; matrix products, arithmetic and copies ran while one was open for 0% of the time, Pallas kernels for 1%

profile of v5, /device:TPU:1, one launch (start us, length us, event | category | flops | bytes accessed | tf_op | source)
XLA Modules:
  0.0 52.2 jit_solution(18272041214926508833)
XLA Ops:
  0.0 1.7 %shard_map.37 = (f32[576,128]{1,0:T(8,128)S(1)}, f32[4,432,128]{2,1,0:T(8,128)S(1)}, bf16[2,2,192,256]{3,2,1,0:T(8,128)(2,1)S(1)}) custom-call(f32[8,15488]{1,0:T(8,128)} %x_ref.1, bf16[2,2,192,256]{3,2,1,0:T(8,128)(2,1)} %constant.4.clone.table_ref), custom_call_target="tpu_custom_call" | custom-call | tf_op jit(solution)/shard_map/pallas_call | solution.py:376
  1.7 1.5 %collective-permute-start = (f32[576,128]{1,0:T(8,128)S(1)}, f32[576,128]{1,0:T(8,128)S(1)}, u32[]{:S(2)}, u32[]{:S(2)}) collective-permute-start(f32[576,128]{1,0:T(8,128)S(1)} %get-tuple-element.10), channel_id=1, source_target_pairs={{0,1},{1,0},{2,3},{3,2},{4,5},{5,4},{6,7},{7,6},{8,9},{9,8},{10,11... | collective-permute-start | bytes 884744 | tf_op jit(solution)/shard_map/ppermute | solution.py:353
  3.2 0.4 shard_map.38.own_ref
  3.5 0.8 %collective-permute-done.other_ref = f32[576,128]{1,0:T(8,128)S(1)} collective-permute-done((f32[576,128]{1,0:T(8,128)S(1)}, f32[576,128]{1,0:T(8,128)S(1)}, u32[]{:S(2)}, u32[]{:S(2)}) %collective-permute-start) | collective-permute-done | bytes 294944 | tf_op jit(solution)/shard_map/ppermute | solution.py:353
  4.4 0.1 shard_map.39
  4.4 0.0 copy-start.1
  4.4 24.3 %all_to_all.10 = f32[64,1,2304]{2,1,0:T(1,128)S(1)} all-to-all(f32[64,1,2304]{2,1,0:T(1,128)S(1)} %bitcast.6), channel_id=1, replica_groups=mesh['gz'=16,'x'=4,'core'=2] {'gz','x'}, dimensions={0} | all-to-all | bytes 1179648 | tf_op jit(solution)/shard_map/all_to_all | solution.py:348
  28.8 0.0 copy-done.1
  28.8 1.5 %shard_map.40 = f32[1152,128]{1,0:T(8,128)S(1)} custom-call(f32[1152,128]{1,0:T(8,128)S(1)} %bitcast.7, bf16[2,2,256,256]{3,2,1,0:T(8,128)(2,1)S(1)} %copy-done.1), custom_call_target="tpu_custom_call" | custom-call | tf_op jit(solution)/shard_map/pallas_call | solution.py:387
  30.3 16.2 %all_to_all.11 = f32[64,1,2304]{2,1,0:T(1,128)S(1)} all-to-all(f32[64,1,2304]{2,1,0:T(1,128)S(1)} %bitcast.8), channel_id=1, replica_groups=mesh['gz'=16,'x'=4,'core'=2] {'gz','x'}, dimensions={0} | all-to-all | bytes 1179648 | tf_op jit(solution)/shard_map/all_to_all | solution.py:348
  46.5 0.0 copy-start
  46.5 3.2 %collective-permute-start.1 = (f32[576,128]{1,0:T(8,128)S(1)}, f32[576,128]{1,0:T(8,128)S(1)}, u32[]{:S(2)}, u32[]{:S(2)}) collective-permute-start(f32[576,128]{1,0:T(8,128)S(1)} %shard_map.41), channel_id=1, source_target_pairs={{0,1},{1,0},{2,3},{3,2},{4,5},{5,4},{6,7},{7,6},{8,9},{9,8},{10,11... | collective-permute-start | bytes 884744 | tf_op jit(solution)/shard_map/ppermute | solution.py:353
  49.7 0.0 copy-done
  49.7 0.4 shard_map.42.own_ref
  50.0 0.8 %collective-permute-done.1.in_ref = f32[576,128]{1,0:T(8,128)S(1)} collective-permute-done((f32[576,128]{1,0:T(8,128)S(1)}, f32[576,128]{1,0:T(8,128)S(1)}, u32[]{:S(2)}, u32[]{:S(2)}) %collective-permute-start.1) | collective-permute-done | bytes 294944 | tf_op jit(solution)/shard_map/ppermute | solution.py:353
  50.9 1.3 %shard_map.43 = f32[8,15488]{1,0:T(8,128)} custom-call(f32[576,128]{1,0:T(8,128)S(1)} %collective-permute-done.1.in_ref, f32[384,256]{1,0:T(8,128)S(1)} %shard_map.42.own_ref, bf16[2,2,192,256]{3,2,1,0:T(8,128)(2,1)S(1)} %copy-done), custom_call_target="tpu_custom_call" | custom-call | tf_op jit(solution)/shard_map/pallas_call | solution.py:398
  (1 shorter events, 0.0 us)
Async XLA Ops:
  1.7 2.7 %collective-permute-start = (f32[576,128]{1,0:T(8,128)S(1)}, f32[576,128]{1,0:T(8,128)S(1)}, u32[]{:S(2)}, u32[]{:S(2)}) collective-permute-start(f32[576,128]{1,0:T(8,128)S(1)} %get-tuple-element.10), channel_id=1, source_target_pairs={{0,1},{1,0},{2,3},{3,2},{4,5},{5,4},{6,7},{7,6},{8,9},{9,8},{10,11... | collective-permute-start | bytes 884744 | tf_op jit(solution)/shard_map/ppermute | solution.py:353
  4.4 24.3 %copy-start.1 = (bf16[2,2,256,256]{3,2,1,0:T(8,128)(2,1)S(1)}, bf16[2,2,256,256]{3,2,1,0:T(8,128)(2,1)}, u32[]{:S(2)}) copy-start(bf16[2,2,256,256]{3,2,1,0:T(8,128)(2,1)} %constant.5.clone.table_ref) | copy-start | bytes 1572868
  46.5 3.2 %copy-start = (bf16[2,2,192,256]{3,2,1,0:T(8,128)(2,1)S(1)}, bf16[2,2,192,256]{3,2,1,0:T(8,128)(2,1)}, u32[]{:S(2)}) copy-start(bf16[2,2,192,256]{3,2,1,0:T(8,128)(2,1)} %constant.4.clone.table_ref) | copy-start | bytes 1179652
  46.5 4.4 %collective-permute-start.1 = (f32[576,128]{1,0:T(8,128)S(1)}, f32[576,128]{1,0:T(8,128)S(1)}, u32[]{:S(2)}, u32[]{:S(2)}) collective-permute-start(f32[576,128]{1,0:T(8,128)S(1)} %shard_map.41), channel_id=1, source_target_pairs={{0,1},{1,0},{2,3},{3,2},{4,5},{5,4},{6,7},{7,6},{8,9},{9,8},{10,11... | collective-permute-start | bytes 884744 | tf_op jit(solution)/shard_map/ppermute | solution.py:353

commit v6 on v4

--- a/solution.py
+++ b/solution.py
@@ -6,6 +6,7 @@
 from jax import lax
 from jax.experimental import pallas as pl
 from jax.experimental.pallas import tpu as pltpu
+from jax.sharding import Mesh
 from jax.sharding import PartitionSpec as P
 
 NX = 352
@@ -20,11 +21,14 @@
 SLOT = PAD // 2
 PAIR = 2 * LANES
 GZ = 16
-GY = 8
+GX = 4
+CORES = 2
+GY = GX * CORES
 PLANES = 8
 ROWS = NY // GY
 CHUNK = PAD // GY
 PITCH = PLANES + 1
+BLOCKS = (0, 16, 32, CHUNK)
 PARTS = (0, 24, ROWS)
 OWN = 3
 PEERS = GZ * GY
@@ -191,8 +195,8 @@
 
 
 def kappa_tile(own, j):
-    device = lax.axis_index("gz") * GY + lax.axis_index("gy")
-    index_x = jnp.full((GZ, LANES), device * OWN + own, jnp.int32)
+    place = (lax.axis_index("core") * GZ + lax.axis_index("gz")) * GX + lax.axis_index("x")
+    index_x = jnp.full((GZ, LANES), place * OWN + own, jnp.int32)
     index_y = lax.broadcasted_iota(jnp.int32, (GZ, LANES), 1) + j * LANES
     wave_x = wavenumber(index_x, NX)
     wave_y = wavenumber(index_y, NY)
@@ -200,7 +204,9 @@
 
 
 def message_row(half, g, own, j):
-    return pl.ds((half * 8 * GY + g) * BELONG + own * TILES + j, 8, stride=GY * BELONG)
+    x, core = divmod(g, CORES)
+    first = ((core * GZ + half * 8) * GX + x) * BELONG + own * TILES + j
+    return pl.ds(first, 8, stride=GX * BELONG)
 
 
 def middle(in_ref, table_ref, out_ref, work_ref, phi_ref):
@@ -221,15 +227,13 @@
             decay = jnp.exp(-kappa)
             scale = 0.5 / kappa
             hat = [phi_ref[pl.ds(z * block + own * GZ, GZ), lane_tile(j)] for z in range(PLANES)]
-            up = [hat[0]]
+            over = hat[0]
             for z in range(1, PLANES):
-                up.append(decay * up[-1] + hat[z])
-            down = [jnp.zeros((GZ, LANES), F32)]
-            for z in range(PLANES - 1, 0, -1):
-                down.append(decay * (down[-1] + hat[z]))
-            down = down[::-1]
-            over = up[-1]
-            under = decay * (down[0] + hat[0])
+                over = decay * over + hat[z]
+            under = hat[-1]
+            for z in range(PLANES - 2, -1, -1):
+                under = decay * under + hat[z]
+            under = decay * under
             power = decay * decay
             power = power * power
             power = power * power
@@ -241,14 +245,13 @@
                 step *= 2
             over = jnp.where(gz >= 1, pltpu.roll(over, 1, 0), 0.0)
             under = jnp.where(gz < GZ - 1, pltpu.roll(under, GZ - 1, 0), 0.0)
+            down = []
+            for z in range(PLANES - 1, -1, -1):
+                down.append(under)
+                under = decay * (under + hat[z])
             for z in range(PLANES):
-                over = decay * over
-                up[z] = up[z] + over
-            for z in range(PLANES - 1, -1, -1):
-                down[z] = down[z] + under
-                under = decay * under
-            for z in range(PLANES):
-                phi_ref[pl.ds(z * block + own * GZ, GZ), lane_tile(j)] = (up[z] + down[z]) * scale
+                over = decay * over + hat[z]
+                phi_ref[pl.ds(z * block + own * GZ, GZ), lane_tile(j)] = (over + down[PLANES - 1 - z]) * scale
 
     both_parities(phi_ref, table_ref, ((1,), (0,)), work_ref)
     for tile in range(block // 8):
@@ -262,47 +265,50 @@
 
 
 def backward_x(in_ref, table_ref, out_ref, field_ref, flat_ref, sems):
-    parts = []
+    lane = lax.broadcasted_iota(jnp.int32, (PLANES, LANES), 1)
+    turned = []
     for parity in range(2):
         rows = [pl.ds(parity * SLOT * TILES + j, SLOT, stride=TILES) for j in range(TILES)]
-        value = jnp.concatenate([in_ref[row, :] for row in rows], axis=1)
-        parts.append(product(split(jnp.transpose(value)), table_of(table_ref, parity), ((1,), (0,))))
-    for side, value in enumerate((parts[0] + parts[1], parts[0] - parts[1])):
-        for j in range(2):
-            for z in range(PLANES):
-                for y in range(0, CHUNK, 8):
-                    rows = pl.ds(z + y * PITCH, 8, stride=PITCH)
-                    field_ref[2 * side + j, rows, :] = value[z * CHUNK + y : z * CHUNK + y + 8, lane_tile(j)]
-    lane = lax.broadcasted_iota(jnp.int32, (PLANES, LANES), 1)
+        turned.append(jnp.transpose(jnp.concatenate([in_ref[row, :] for row in rows], axis=1)))
     stores = []
     carry = None
-    for piece in range(2 * ROWS):
-        y, side = divmod(piece, 2)
-        offset = piece * HALF
-        shift = offset % LANES
-        end = shift + HALF
-        tiles = [field_ref[2 * side + j, pl.ds(y * PITCH, PLANES), :] for j in range(2)]
-        if end > PAIR:
-            tiles.append(jnp.zeros((PLANES, LANES), F32))
-        tiles = shift_lanes(tiles, shift, lane)
-        if carry is not None:
-            tiles[0] = tiles[0] + carry
-        full = end // LANES
-        carry = tiles[full] if end % LANES else None
-        for j in range(full):
-            flat_ref[:, pl.ds(offset - shift + j * LANES, LANES)] = tiles[j]
-        if side == 1 and y + 1 in PARTS:
-            n = PARTS.index(y + 1) - 1
-            part = pl.ds(PARTS[n] * NX, (y + 1 - PARTS[n]) * NX)
-            stores.append(pltpu.make_async_copy(flat_ref.at[:, part], out_ref.at[:, part], sems.at[n]))
-            stores[-1].start()
+    for n, (first, last) in enumerate(zip(BLOCKS, BLOCKS[1:])):
+        tops = [z * CHUNK + y for z in range(PLANES) for y in range(first, last, 8)]
+        parts = []
+        for parity in range(2):
+            value = jnp.concatenate([turned[parity][t : t + 8] for t in tops], axis=0)
+            parts.append(product(split(value), table_of(table_ref, parity), ((1,), (0,))))
+        for side, value in enumerate((parts[0] + parts[1], parts[0] - parts[1])):
+            for j in range(2):
+                for i, t in enumerate(tops):
+                    z, y = divmod(t, CHUNK)
+                    rows = pl.ds(z + y * PITCH, 8, stride=PITCH)
+                    field_ref[2 * side + j, rows, :] = value[8 * i : 8 * i + 8, lane_tile(j)]
+        for piece in range(2 * first, 2 * min(last, ROWS)):
+            y, side = divmod(piece, 2)
+            offset = piece * HALF
+            shift = offset % LANES
+            end = shift + HALF
+            tiles = [field_ref[2 * side + j, pl.ds(y * PITCH, PLANES), :] for j in range(2)]
+            if end > PAIR:
+                tiles.append(jnp.zeros((PLANES, LANES), F32))
+            tiles = shift_lanes(tiles, shift, lane)
+            if carry is not None:
+                tiles[0] = tiles[0] + carry
+            full = end // LANES
+            carry = tiles[full] if end % LANES else None
+            for j in range(full):
+                flat_ref[:, pl.ds(offset - shift + j * LANES, LANES)] = tiles[j]
+        part = pl.ds(first * NX, (min(last, ROWS) - first) * NX)
+        stores.append(pltpu.make_async_copy(flat_ref.at[:, part], out_ref.at[:, part], sems.at[n]))
+        stores[-1].start()
     for store in stores:
         store.wait()
 
 
 def exchange(buffer):
     whole = buffer.reshape(PEERS, 1, BELONG * LANES)
-    whole = lax.all_to_all(whole, ("gz", "gy"), 0, 0, tiled=True)
+    whole = lax.all_to_all(whole, ("core", "gz", "x"), 0, 0, tiled=True)
     return whole.reshape(SEND, LANES)
 
 
@@ -345,15 +351,17 @@
         out_shape=jax.ShapeDtypeStruct(density.shape, F32),
         in_specs=[vmem, vmem],
         out_specs=hbm,
-        scratch_shapes=[field, flat, groups],
+        scratch_shapes=[field, flat, pltpu.SemaphoreType.DMA((len(BLOCKS) - 1,))],
     )(here(exchange(back)), here(table_x))
 
 
 def solution(mesh):
+    split_rows = Mesh(mesh.devices.reshape(GZ, GX, CORES), ("gz", "x", "core"))
+    spec = P("gz", ("x", "core"))
     return jax.shard_map(
         on_device,
-        mesh=mesh,
-        in_specs=(P("gz", "gy"),),
-        out_specs=P("gz", "gy"),
+        mesh=split_rows,
+        in_specs=(spec,),
+        out_specs=spec,
         check_vma=False,
     )

time: 49.5 us -> 48.6 us (0.982)
  blocking collectives: 44.3 us -> 43.7 us
    all_to_all x2, blocking collectives: 44.3 us -> 43.7 us  [exchange(): whole = lax.all_to_all(whole, ('core', 'gz', 'x'), 0, 0, tiled=True)]
where the time goes in v6:
time: 48.6 us; the launch traced here: 48.5 us
  blocking collectives  43.7 us (90%)
  Pallas kernels  4.75 us (10%)
    all_to_all x2, blocking collectives, exchange(): whole = lax.all_to_all(whole, ('core', 'gz', 'x'), 0, 0, tiled=True)  43.7 us
    pallas_call x1, Pallas kernels, on_device(): pl.pallas_call(forward_x, out_shape=message, in_specs=[hbm, hbm], out_spe...  1.86 us
    pallas_call x1, Pallas kernels, on_device(): pl.pallas_call(backward_x, out_shape=jax.ShapeDtypeStruct(density.shape,...  1.48 us
    pallas_call x1, Pallas kernels, on_device(): pl.pallas_call(middle, out_shape=message, in_specs=[vmem, vmem], out_spec...  1.42 us

profile of v6, /device:TPU:1, one launch (start us, length us, event | category | flops | bytes accessed | tf_op | source)
XLA Modules:
  0.0 48.5 jit_solution(5700220009955866377)
XLA Ops:
  0.0 1.9 %shard_map.37 = f32[1152,128]{1,0:T(8,128)S(1)} custom-call(f32[8,15488]{1,0:T(8,128)} %x_ref.1, bf16[2,2,192,256]{3,2,1,0:T(8,128)(2,1)} %constant.4.clone.table_ref), custom_call_target="tpu_custom_call" | custom-call | tf_op jit(solution)/shard_map/pallas_call | solution.py:329
  1.9 0.0 copy-start.1
  1.9 25.5 %all_to_all.10 = f32[128,1,1152]{2,1,0:T(1,128)S(1)} all-to-all(f32[128,1,1152]{2,1,0:T(1,128)S(1)} %bitcast.7), channel_id=1, replica_groups=mesh['gz'=16,'x'=4,'core'=2] {'core','gz','x'}, dimensions={0} | all-to-all | bytes 1179648 | tf_op jit(solution)/shard_map/all_to_all | solution.py:311
  27.3 0.0 copy-done.1
  27.3 1.4 %shard_map.38 = f32[1152,128]{1,0:T(8,128)S(1)} custom-call(f32[1152,128]{1,0:T(8,128)S(1)} %bitcast.4, bf16[2,2,256,256]{3,2,1,0:T(8,128)(2,1)S(1)} %copy-done.1), custom_call_target="tpu_custom_call" | custom-call | tf_op jit(solution)/shard_map/pallas_call | solution.py:342
  28.8 0.0 copy-start
  28.8 18.2 %all_to_all.11 = f32[128,1,1152]{2,1,0:T(1,128)S(1)} all-to-all(f32[128,1,1152]{2,1,0:T(1,128)S(1)} %bitcast.5), channel_id=1, replica_groups=mesh['gz'=16,'x'=4,'core'=2] {'core','gz','x'}, dimensions={0} | all-to-all | bytes 1179648 | tf_op jit(solution)/shard_map/all_to_all | solution.py:311
  47.0 0.0 copy-done
  47.0 1.5 %shard_map.39 = f32[8,15488]{1,0:T(8,128)} custom-call(f32[1152,128]{1,0:T(8,128)S(1)} %bitcast.6, bf16[2,2,192,256]{3,2,1,0:T(8,128)(2,1)S(1)} %copy-done), custom_call_target="tpu_custom_call" | custom-call | tf_op jit(solution)/shard_map/pallas_call | solution.py:349
Async XLA Ops:
  1.9 25.5 %copy-start.1 = (bf16[2,2,256,256]{3,2,1,0:T(8,128)(2,1)S(1)}, bf16[2,2,256,256]{3,2,1,0:T(8,128)(2,1)}, u32[]{:S(2)}) copy-start(bf16[2,2,256,256]{3,2,1,0:T(8,128)(2,1)} %constant.5.clone.table_ref) | copy-start | bytes 1572868
  28.8 18.2 %copy-start = (bf16[2,2,192,256]{3,2,1,0:T(8,128)(2,1)S(1)}, bf16[2,2,192,256]{3,2,1,0:T(8,128)(2,1)}, u32[]{:S(2)}) copy-start(bf16[2,2,192,256]{3,2,1,0:T(8,128)(2,1)} %constant.4.clone.table_ref) | copy-start | bytes 1179652

commit v7 on v6

--- a/solution.py
+++ b/solution.py
@@ -118,7 +118,7 @@
     return shift_lanes(tiles, -shift, lane)[:2]
 
 
-def forward_x(x_ref, table_ref, out_ref, field_ref, flat_ref, local_ref, x_sems, table_sem):
+def forward_x(x_ref, table_ref, out_ref, decay_ref, scale_ref, field_ref, flat_ref, local_ref, x_sems, table_sem):
     lane = lax.broadcasted_iota(jnp.int32, (PLANES, LANES), 1)
     loads = []
     for n, (first, last) in enumerate(zip(PARTS, PARTS[1:])):
@@ -128,6 +128,11 @@
     for load in loads:
         load.start()
     table_load.start()
+    for own in range(OWN):
+        for j in range(TILES):
+            kappa = kappa_tile(own, j)
+            decay_ref[pl.ds(8 * own, 8), lane_tile(j)] = jnp.exp(-kappa)
+            scale_ref[pl.ds(8 * own, 8), lane_tile(j)] = 0.5 / kappa
     for y in range(ROWS, CHUNK):
         for j in range(4):
             field_ref[j, pl.ds(y * PITCH, PLANES), :] = jnp.zeros((PLANES, LANES), F32)
@@ -180,12 +185,12 @@
     return [[a + b for a, b in p] for p in pairs] + [[a - b for a, b in p] for p in pairs]
 
 
-def both_parities(value_ref, table_ref, dims, out_ref):
-    even = product(split(value_ref[:, :PAIR]), table_of(table_ref, 0), dims)
-    odd = product(split(value_ref[:, PAD - PAIR :]), table_of(table_ref, 1), dims)
-    out_ref[:, lane_tile(0)] = even[:, :LANES]
-    out_ref[:, lane_tile(1)] = even[:, LANES:] + odd[:, :LANES]
-    out_ref[:, lane_tile(2)] = odd[:, LANES:]
+def both_parities(value_ref, table_ref, dims, out_ref, rows):
+    even = product(split(value_ref[rows, :PAIR]), table_of(table_ref, 0), dims)
+    odd = product(split(value_ref[rows, PAD - PAIR :]), table_of(table_ref, 1), dims)
+    out_ref[rows, lane_tile(0)] = even[:, :LANES]
+    out_ref[rows, lane_tile(1)] = even[:, LANES:] + odd[:, :LANES]
+    out_ref[rows, lane_tile(2)] = odd[:, LANES:]
 
 
 def wavenumber(index, length):
@@ -196,8 +201,8 @@
 
 def kappa_tile(own, j):
     place = (lax.axis_index("core") * GZ + lax.axis_index("gz")) * GX + lax.axis_index("x")
-    index_x = jnp.full((GZ, LANES), place * OWN + own, jnp.int32)
-    index_y = lax.broadcasted_iota(jnp.int32, (GZ, LANES), 1) + j * LANES
+    index_x = jnp.full((8, LANES), place * OWN + own, jnp.int32)
+    index_y = lax.broadcasted_iota(jnp.int32, (8, LANES), 1) + j * LANES
     wave_x = wavenumber(index_x, NX)
     wave_y = wavenumber(index_y, NY)
     return jnp.sqrt(1.0 / (SCREEN * SCREEN) + wave_x * wave_x + wave_y * wave_y)
@@ -209,59 +214,85 @@
     return pl.ds(first, 8, stride=GX * BELONG)
 
 
-def middle(in_ref, table_ref, out_ref, work_ref, phi_ref):
-    lane = lax.broadcasted_iota(jnp.int32, (8, LANES), 1)
-    block = OWN * GZ
-    for tile in range(block // 8):
-        own, half = divmod(tile, GZ // 8)
+def plane_row(own, z, half=0):
+    return own * PLANES * GZ + z * GZ + half * 8
+
+
+def gather(own, lane, in_ref, work_ref):
+    for half in range(GZ // 8):
         arrays = [[in_ref[message_row(half, g, own, j), :] for j in range(TILES)] for g in range(GY)]
         for z, parts in enumerate(swap_chunks(butterfly(arrays), lane)):
             for j in range(TILES):
-                work_ref[pl.ds(z * block + tile * 8, 8), lane_tile(j)] = parts[j]
-    both_parities(work_ref, table_ref, ((1,), (1,)), phi_ref)
-
-    gz = lax.broadcasted_iota(jnp.int32, (GZ, LANES), 0)
-    for own in range(OWN):
-        for j in range(TILES):
-            kappa = kappa_tile(own, j)
-            decay = jnp.exp(-kappa)
-            scale = 0.5 / kappa
-            hat = [phi_ref[pl.ds(z * block + own * GZ, GZ), lane_tile(j)] for z in range(PLANES)]
-            over = hat[0]
-            for z in range(1, PLANES):
-                over = decay * over + hat[z]
-            under = hat[-1]
-            for z in range(PLANES - 2, -1, -1):
-                under = decay * under + hat[z]
-            under = decay * under
-            power = decay * decay
-            power = power * power
-            power = power * power
-            step = 1
-            while step < GZ:
-                over = over + jnp.where(gz >= step, power * pltpu.roll(over, step, 0), 0.0)
-                under = under + jnp.where(gz < GZ - step, power * pltpu.roll(under, GZ - step, 0), 0.0)
-                power = power * power
-                step *= 2
-            over = jnp.where(gz >= 1, pltpu.roll(over, 1, 0), 0.0)
-            under = jnp.where(gz < GZ - 1, pltpu.roll(under, GZ - 1, 0), 0.0)
-            down = []
-            for z in range(PLANES - 1, -1, -1):
-                down.append(under)
-                under = decay * (under + hat[z])
-            for z in range(PLANES):
-                over = decay * over + hat[z]
-                phi_ref[pl.ds(z * block + own * GZ, GZ), lane_tile(j)] = (over + down[PLANES - 1 - z]) * scale
-
-    both_parities(phi_ref, table_ref, ((1,), (0,)), work_ref)
-    for tile in range(block // 8):
-        own, half = divmod(tile, GZ // 8)
+                work_ref[pl.ds(plane_row(own, z, half), 8), lane_tile(j)] = parts[j]
+
+
+def scatter(own, lane, work_ref, out_ref):
+    for half in range(GZ // 8):
         arrays = [
-            [work_ref[pl.ds(z * block + tile * 8, 8), lane_tile(j)] for j in range(TILES)] for z in range(PLANES)
+            [work_ref[pl.ds(plane_row(own, z, half), 8), lane_tile(j)] for j in range(TILES)] for z in range(PLANES)
         ]
         for g, parts in enumerate(butterfly(swap_chunks(arrays, lane))):
             for j in range(TILES):
                 out_ref[message_row(half, g, own, j), :] = parts[j]
+
+
+def decaying_sums(own, gz, decay_ref, scale_ref, phi_ref):
+    for j in range(TILES):
+        decay = decay_ref[pl.ds(8 * own, 8), lane_tile(j)]
+        scale = scale_ref[pl.ds(8 * own, 8), lane_tile(j)]
+        power = decay * decay
+        power = power * power
+        power = power * power
+        decay, scale, power = (jnp.concatenate([t] * (GZ // 8), axis=0) for t in (decay, scale, power))
+        hat = [phi_ref[pl.ds(plane_row(own, z), GZ), lane_tile(j)] for z in range(PLANES)]
+        over = hat[0]
+        for z in range(1, PLANES):
+            over = decay * over + hat[z]
+        under = hat[-1]
+        for z in range(PLANES - 2, -1, -1):
+            under = decay * under + hat[z]
+        under = decay * under
+        step = 1
+        while step < GZ:
+            over = over + jnp.where(gz >= step, power * pltpu.roll(over, step, 0), 0.0)
+            under = under + jnp.where(gz < GZ - step, power * pltpu.roll(under, GZ - step, 0), 0.0)
+            power = power * power
+            step *= 2
+        over = jnp.where(gz >= 1, pltpu.roll(over, 1, 0), 0.0)
+        under = jnp.where(gz < GZ - 1, pltpu.roll(under, GZ - 1, 0), 0.0)
+        down = []
+        for z in range(PLANES - 1, -1, -1):
+            down.append(under)
+            under = decay * (under + hat[z])
+        for z in range(PLANES):
+            over = decay * over + hat[z]
+            phi_ref[pl.ds(plane_row(own, z), GZ), lane_tile(j)] = (over + down[PLANES - 1 - z]) * scale
+
+
+def middle(in_ref, table_ref, decay_ref, scale_ref, out_ref, work_ref, phi_ref, back_ref):
+    lane = lax.broadcasted_iota(jnp.int32, (8, LANES), 1)
+    gz = lax.broadcasted_iota(jnp.int32, (GZ, LANES), 0)
+    forth = ((1,), (1,))
+    back = ((1,), (0,))
+    every = pl.ds(0, PAD)
+
+    def rows(own):
+        return pl.ds(own * PLANES * GZ, PLANES * GZ)
+
+    first = pl.ds(0, PLANES * GZ)
+    rest = pl.ds(PLANES * GZ, (OWN - 1) * PLANES * GZ)
+    for own in range(OWN):
+        gather(own, lane, in_ref, work_ref)
+    both_parities(work_ref, table_ref, forth, phi_ref, first)
+    both_parities(work_ref, table_ref, forth, phi_ref, rest)
+    decaying_sums(0, gz, decay_ref, scale_ref, phi_ref)
+    both_parities(phi_ref, table_ref, back, back_ref, first)
+    decaying_sums(1, gz, decay_ref, scale_ref, phi_ref)
+    decaying_sums(2, gz, decay_ref, scale_ref, phi_ref)
+    scatter(0, lane, back_ref, out_ref)
+    both_parities(phi_ref, table_ref, back, back_ref, rest)
+    scatter(1, lane, back_ref, out_ref)
+    scatter(2, lane, back_ref, out_ref)
 
 
 def backward_x(in_ref, table_ref, out_ref, field_ref, flat_ref, sems):
@@ -326,11 +357,12 @@
     def here(value):
         return pltpu.with_memory_space_constraint(value, pltpu.VMEM)
 
-    sent = pl.pallas_call(
+    factors = pltpu.VMEM((8 * OWN, PAD), F32)
+    sent, decay, scale = pl.pallas_call(
         forward_x,
-        out_shape=message,
+        out_shape=(message, factors, factors),
         in_specs=[hbm, hbm],
-        out_specs=vmem,
+        out_specs=(vmem, vmem, vmem),
         scratch_shapes=[
             field,
             flat,
@@ -342,10 +374,10 @@
     back = pl.pallas_call(
         middle,
         out_shape=message,
-        in_specs=[vmem, vmem],
+        in_specs=[vmem, vmem, vmem, vmem],
         out_specs=vmem,
-        scratch_shapes=[square, square],
-    )(here(exchange(sent)), here(table_y))
+        scratch_shapes=[square, square, square],
+    )(here(exchange(sent)), here(table_y), here(decay), here(scale))
     return pl.pallas_call(
         backward_x,
         out_shape=jax.ShapeDtypeStruct(density.shape, F32),

time: 48.6 us -> 48.6 us (level)
  no operation moved by 1% of the time
where the time goes in v7:
time: 48.6 us; the launch traced here: 48.4 us
  blocking collectives  43.7 us (90%)
  Pallas kernels  4.66 us (10%)
    all_to_all x2, blocking collectives, exchange(): whole = lax.all_to_all(whole, ('core', 'gz', 'x'), 0, 0, tiled=True)  43.7 us
    pallas_call x1, Pallas kernels, on_device(): pl.pallas_call(forward_x, out_shape=(message, factors, factors), in_specs...  1.86 us
    pallas_call x1, Pallas kernels, on_device(): pl.pallas_call(backward_x, out_shape=jax.ShapeDtypeStruct(density.shape,...  1.48 us
    pallas_call x1, Pallas kernels, on_device(): pl.pallas_call(middle, out_shape=message, in_specs=[vmem, vmem, vmem, vme...  1.33 us

profile of v7, /device:TPU:1, one launch (start us, length us, event | category | flops | bytes accessed | tf_op | source)
XLA Modules:
  0.0 48.4 jit_solution(8155536668188564923)
XLA Ops:
  0.0 1.9 %shard_map.37 = (f32[1152,128]{1,0:T(8,128)S(1)}, f32[24,384]{1,0:T(8,128)S(1)}, f32[24,384]{1,0:T(8,128)S(1)}) custom-call(f32[8,15488]{1,0:T(8,128)} %x_ref.1, bf16[2,2,192,256]{3,2,1,0:T(8,128)(2,1)} %constant.4.clone.table_ref), custom_call_target="tpu_custom_call" | custom-call | tf_op jit(solution)/shard_map/pallas_call | solution.py:361
  1.9 0.0 copy-start.1
  1.9 25.5 %all_to_all.10 = f32[128,1,1152]{2,1,0:T(1,128)S(1)} all-to-all(f32[128,1,1152]{2,1,0:T(1,128)S(1)} %bitcast.7), channel_id=1, replica_groups=mesh['gz'=16,'x'=4,'core'=2] {'core','gz','x'}, dimensions={0} | all-to-all | bytes 1179648 | tf_op jit(solution)/shard_map/all_to_all | solution.py:342
  27.3 0.0 copy-done.1
  27.3 1.3 %shard_map.38 = f32[1152,128]{1,0:T(8,128)S(1)} custom-call(f32[1152,128]{1,0:T(8,128)S(1)} %bitcast.4, bf16[2,2,256,256]{3,2,1,0:T(8,128)(2,1)S(1)} %copy-done.1, f32[24,384]{1,0:T(8,128)S(1)} %get-tuple-element.9.decay_ref, f32[24,384]{1,0:T(8,128)S(1)} %get-tuple-element.10.scale_ref), custom_call_target="tpu_custom_call" | custom-call | tf_op jit(solution)/shard_map/pallas_call | solution.py:374
  28.7 0.0 copy-start
  28.7 18.2 %all_to_all.11 = f32[128,1,1152]{2,1,0:T(1,128)S(1)} all-to-all(f32[128,1,1152]{2,1,0:T(1,128)S(1)} %bitcast.5), channel_id=1, replica_groups=mesh['gz'=16,'x'=4,'core'=2] {'core','gz','x'}, dimensions={0} | all-to-all | bytes 1179648 | tf_op jit(solution)/shard_map/all_to_all | solution.py:342
  46.9 0.0 copy-done
  46.9 1.5 %shard_map.39 = f32[8,15488]{1,0:T(8,128)} custom-call(f32[1152,128]{1,0:T(8,128)S(1)} %bitcast.6, bf16[2,2,192,256]{3,2,1,0:T(8,128)(2,1)S(1)} %copy-done), custom_call_target="tpu_custom_call" | custom-call | tf_op jit(solution)/shard_map/pallas_call | solution.py:381
Async XLA Ops:
  1.9 25.5 %copy-start.1 = (bf16[2,2,256,256]{3,2,1,0:T(8,128)(2,1)S(1)}, bf16[2,2,256,256]{3,2,1,0:T(8,128)(2,1)}, u32[]{:S(2)}) copy-start(bf16[2,2,256,256]{3,2,1,0:T(8,128)(2,1)} %constant.5.clone.table_ref) | copy-start | bytes 1572868
  28.7 18.2 %copy-start = (bf16[2,2,192,256]{3,2,1,0:T(8,128)(2,1)S(1)}, bf16[2,2,192,256]{3,2,1,0:T(8,128)(2,1)}, u32[]{:S(2)}) copy-start(bf16[2,2,192,256]{3,2,1,0:T(8,128)(2,1)} %constant.4.clone.table_ref) | copy-start | bytes 1179652

commit v8 on v7

--- a/solution.py
+++ b/solution.py
@@ -69,6 +69,14 @@
 def x_table():
     table = np.zeros((2, SLOT, PAIR))
     table[:, :HALF, :HALF] = half_basis(NX)
+    return halves(table)
+
+
+def x_back_table():
+    table = np.zeros((2, PAIR, PAIR))
+    basis = half_basis(NX)
+    table[0, :HALF, :HALF] = basis[0]
+    table[1, PAIR - SLOT : PAIR - SLOT + HALF, :HALF] = basis[1]
     return halves(table)
 
 
@@ -297,10 +305,9 @@
 
 def backward_x(in_ref, table_ref, out_ref, field_ref, flat_ref, sems):
     lane = lax.broadcasted_iota(jnp.int32, (PLANES, LANES), 1)
-    turned = []
-    for parity in range(2):
-        rows = [pl.ds(parity * SLOT * TILES + j, SLOT, stride=TILES) for j in range(TILES)]
-        turned.append(jnp.transpose(jnp.concatenate([in_ref[row, :] for row in rows], axis=1)))
+    whole = jnp.concatenate([in_ref[pl.ds(j, PAD, stride=TILES), :] for j in range(TILES)], axis=1)
+    whole = jnp.transpose(whole)
+    turned = [whole[:, :PAIR], whole[:, PAD - PAIR :]]
     stores = []
     carry = None
     for n, (first, last) in enumerate(zip(BLOCKS, BLOCKS[1:])):
@@ -384,7 +391,7 @@
         in_specs=[vmem, vmem],
         out_specs=hbm,
         scratch_shapes=[field, flat, pltpu.SemaphoreType.DMA((len(BLOCKS) - 1,))],
-    )(here(exchange(back)), here(table_x))
+    )(here(exchange(back)), here(jnp.asarray(x_back_table())))
 
 
 def solution(mesh):

time: 48.6 us -> 48.5 us (level)
  no operation moved by 1% of the time
where the time goes in v8:
time: 48.5 us; the launch traced here: 48.3 us
  blocking collectives  43.7 us (90%)
  Pallas kernels  4.61 us (10%)
    all_to_all x2, blocking collectives, exchange(): whole = lax.all_to_all(whole, ('core', 'gz', 'x'), 0, 0, tiled=True)  43.7 us
    pallas_call x1, Pallas kernels, on_device(): pl.pallas_call(forward_x, out_shape=(message, factors, factors), in_specs...  1.86 us
    pallas_call x1, Pallas kernels, on_device(): pl.pallas_call(backward_x, out_shape=jax.ShapeDtypeStruct(density.shape,...  1.42 us
    pallas_call x1, Pallas kernels, on_device(): pl.pallas_call(middle, out_shape=message, in_specs=[vmem, vmem, vmem, vme...  1.33 us

profile of v8, /device:TPU:1, one launch (start us, length us, event | category | flops | bytes accessed | tf_op | source)
XLA Modules:
  0.0 48.3 jit_solution(11480155308768059840)
XLA Ops:
  0.0 1.9 %shard_map.46 = (f32[1152,128]{1,0:T(8,128)S(1)}, f32[24,384]{1,0:T(8,128)S(1)}, f32[24,384]{1,0:T(8,128)S(1)}) custom-call(f32[8,15488]{1,0:T(8,128)} %x_ref.1, bf16[2,2,192,256]{3,2,1,0:T(8,128)(2,1)} %constant.6.clone.table_ref), custom_call_target="tpu_custom_call" | custom-call | tf_op jit(solution)/shard_map/pallas_call | solution.py:368
  1.9 0.0 copy-start.1
  1.9 25.5 %all_to_all.10 = f32[128,1,1152]{2,1,0:T(1,128)S(1)} all-to-all(f32[128,1,1152]{2,1,0:T(1,128)S(1)} %bitcast.7), channel_id=1, replica_groups=mesh['gz'=16,'x'=4,'core'=2] {'core','gz','x'}, dimensions={0} | all-to-all | bytes 1179648 | tf_op jit(solution)/shard_map/all_to_all | solution.py:349
  27.3 0.0 copy-done.1
  27.3 1.3 %shard_map.47 = f32[1152,128]{1,0:T(8,128)S(1)} custom-call(f32[1152,128]{1,0:T(8,128)S(1)} %bitcast.4, bf16[2,2,256,256]{3,2,1,0:T(8,128)(2,1)S(1)} %copy-done.1, f32[24,384]{1,0:T(8,128)S(1)} %get-tuple-element.9.decay_ref, f32[24,384]{1,0:T(8,128)S(1)} %get-tuple-element.10.scale_ref), custom_call_target="tpu_custom_call" | custom-call | tf_op jit(solution)/shard_map/pallas_call | solution.py:381
  28.7 0.0 copy-start
  28.7 18.2 %all_to_all.11 = f32[128,1,1152]{2,1,0:T(1,128)S(1)} all-to-all(f32[128,1,1152]{2,1,0:T(1,128)S(1)} %bitcast.5), channel_id=1, replica_groups=mesh['gz'=16,'x'=4,'core'=2] {'core','gz','x'}, dimensions={0} | all-to-all | bytes 1179648 | tf_op jit(solution)/shard_map/all_to_all | solution.py:349
  46.9 0.0 copy-done
  46.9 1.4 %shard_map.48 = f32[8,15488]{1,0:T(8,128)} custom-call(f32[1152,128]{1,0:T(8,128)S(1)} %bitcast.6, bf16[2,2,256,256]{3,2,1,0:T(8,128)(2,1)S(1)} %copy-done), custom_call_target="tpu_custom_call" | custom-call | tf_op jit(solution)/shard_map/pallas_call | solution.py:388
Async XLA Ops:
  1.9 25.5 %copy-start.1 = (bf16[2,2,256,256]{3,2,1,0:T(8,128)(2,1)S(1)}, bf16[2,2,256,256]{3,2,1,0:T(8,128)(2,1)}, u32[]{:S(2)}) copy-start(bf16[2,2,256,256]{3,2,1,0:T(8,128)(2,1)} %constant.7.clone.table_ref) | copy-start | bytes 1572868
  28.7 18.2 %copy-start = (bf16[2,2,256,256]{3,2,1,0:T(8,128)(2,1)S(1)}, bf16[2,2,256,256]{3,2,1,0:T(8,128)(2,1)}, u32[]{:S(2)}) copy-start(bf16[2,2,256,256]{3,2,1,0:T(8,128)(2,1)} %constant.8.clone.table_ref) | copy-start | bytes 1572868

commit v9 on v8

--- a/solution.py
+++ b/solution.py
@@ -99,7 +99,9 @@
     def dot(a, b):
         return lax.dot_general(a, b, (dims, ((), ())), preferred_element_type=F32)
 
-    return dot(left[0], right[0]) + (dot(left[0], right[1]) + dot(left[1], right[0]))
+    count = left[0].shape[0]
+    both = dot(jnp.concatenate(left, axis=0), right[0])
+    return both[:count] + (both[count:] + dot(left[0], right[1]))
 
 
 def lane_tile(j):

time: 48.5 us -> 48.4 us (level)
  no operation moved by 1% of the time
where the time goes in v9:
time: 48.4 us; the launch traced here: 48.2 us
  blocking collectives  43.7 us (90%)
  Pallas kernels  4.46 us (9%)
    all_to_all x2, blocking collectives, exchange(): whole = lax.all_to_all(whole, ('core', 'gz', 'x'), 0, 0, tiled=True)  43.7 us
    pallas_call x1, Pallas kernels, on_device(): pl.pallas_call(forward_x, out_shape=(message, factors, factors), in_specs...  1.81 us
    pallas_call x1, Pallas kernels, on_device(): pl.pallas_call(backward_x, out_shape=jax.ShapeDtypeStruct(density.shape,...  1.42 us
    pallas_call x1, Pallas kernels, on_device(): pl.pallas_call(middle, out_shape=message, in_specs=[vmem, vmem, vmem, vme...  1.24 us

profile of v9, /device:TPU:1, one launch (start us, length us, event | category | flops | bytes accessed | tf_op | source)
XLA Modules:
  0.0 48.2 jit_solution(14274542554173895302)
XLA Ops:
  0.0 1.8 %shard_map.46 = (f32[1152,128]{1,0:T(8,128)S(1)}, f32[24,384]{1,0:T(8,128)S(1)}, f32[24,384]{1,0:T(8,128)S(1)}) custom-call(f32[8,15488]{1,0:T(8,128)} %x_ref.1, bf16[2,2,192,256]{3,2,1,0:T(8,128)(2,1)} %constant.6.clone.table_ref), custom_call_target="tpu_custom_call" | custom-call | tf_op jit(solution)/shard_map/pallas_call | solution.py:370
  1.8 0.0 copy-start.1
  1.8 25.4 %all_to_all.10 = f32[128,1,1152]{2,1,0:T(1,128)S(1)} all-to-all(f32[128,1,1152]{2,1,0:T(1,128)S(1)} %bitcast.7), channel_id=1, replica_groups=mesh['gz'=16,'x'=4,'core'=2] {'core','gz','x'}, dimensions={0} | all-to-all | bytes 1179648 | tf_op jit(solution)/shard_map/all_to_all | solution.py:351
  27.3 0.0 copy-done.1
  27.3 1.2 %shard_map.47 = f32[1152,128]{1,0:T(8,128)S(1)} custom-call(f32[1152,128]{1,0:T(8,128)S(1)} %bitcast.4, bf16[2,2,256,256]{3,2,1,0:T(8,128)(2,1)S(1)} %copy-done.1, f32[24,384]{1,0:T(8,128)S(1)} %get-tuple-element.9.decay_ref, f32[24,384]{1,0:T(8,128)S(1)} %get-tuple-element.10.scale_ref), custom_call_target="tpu_custom_call" | custom-call | tf_op jit(solution)/shard_map/pallas_call | solution.py:383
  28.5 0.0 copy-start
  28.5 18.2 %all_to_all.11 = f32[128,1,1152]{2,1,0:T(1,128)S(1)} all-to-all(f32[128,1,1152]{2,1,0:T(1,128)S(1)} %bitcast.5), channel_id=1, replica_groups=mesh['gz'=16,'x'=4,'core'=2] {'core','gz','x'}, dimensions={0} | all-to-all | bytes 1179648 | tf_op jit(solution)/shard_map/all_to_all | solution.py:351
  46.8 0.0 copy-done
  46.8 1.4 %shard_map.48 = f32[8,15488]{1,0:T(8,128)} custom-call(f32[1152,128]{1,0:T(8,128)S(1)} %bitcast.6, bf16[2,2,256,256]{3,2,1,0:T(8,128)(2,1)S(1)} %copy-done), custom_call_target="tpu_custom_call" | custom-call | tf_op jit(solution)/shard_map/pallas_call | solution.py:390
Async XLA Ops:
  1.8 25.5 %copy-start.1 = (bf16[2,2,256,256]{3,2,1,0:T(8,128)(2,1)S(1)}, bf16[2,2,256,256]{3,2,1,0:T(8,128)(2,1)}, u32[]{:S(2)}) copy-start(bf16[2,2,256,256]{3,2,1,0:T(8,128)(2,1)} %constant.7.clone.table_ref) | copy-start | bytes 1572868
  28.5 18.2 %copy-start = (bf16[2,2,256,256]{3,2,1,0:T(8,128)(2,1)S(1)}, bf16[2,2,256,256]{3,2,1,0:T(8,128)(2,1)}, u32[]{:S(2)}) copy-start(bf16[2,2,256,256]{3,2,1,0:T(8,128)(2,1)} %constant.8.clone.table_ref) | copy-start | bytes 1572868

commit v10 on v9

--- a/solution.py
+++ b/solution.py
@@ -279,10 +279,9 @@
             phi_ref[pl.ds(plane_row(own, z), GZ), lane_tile(j)] = (over + down[PLANES - 1 - z]) * scale
 
 
-def middle(in_ref, table_ref, decay_ref, scale_ref, out_ref, work_ref, phi_ref, back_ref):
+def middle(in_ref, turned_ref, table_ref, decay_ref, scale_ref, out_ref, work_ref, phi_ref, back_ref):
     lane = lax.broadcasted_iota(jnp.int32, (8, LANES), 1)
     gz = lax.broadcasted_iota(jnp.int32, (GZ, LANES), 0)
-    forth = ((1,), (1,))
     back = ((1,), (0,))
     every = pl.ds(0, PAD)
 
@@ -293,8 +292,8 @@
     rest = pl.ds(PLANES * GZ, (OWN - 1) * PLANES * GZ)
     for own in range(OWN):
         gather(own, lane, in_ref, work_ref)
-    both_parities(work_ref, table_ref, forth, phi_ref, first)
-    both_parities(work_ref, table_ref, forth, phi_ref, rest)
+    both_parities(work_ref, turned_ref, back, phi_ref, first)
+    both_parities(work_ref, turned_ref, back, phi_ref, rest)
     decaying_sums(0, gz, decay_ref, scale_ref, phi_ref)
     both_parities(phi_ref, table_ref, back, back_ref, first)
     decaying_sums(1, gz, decay_ref, scale_ref, phi_ref)
@@ -383,10 +382,10 @@
     back = pl.pallas_call(
         middle,
         out_shape=message,
-        in_specs=[vmem, vmem, vmem, vmem],
+        in_specs=[vmem] * 5,
         out_specs=vmem,
         scratch_shapes=[square, square, square],
-    )(here(exchange(sent)), here(table_y), here(decay), here(scale))
+    )(here(exchange(sent)), here(jnp.asarray(np.swapaxes(y_table(), 2, 3))), here(table_y), here(decay), here(scale))
     return pl.pallas_call(
         backward_x,
         out_shape=jax.ShapeDtypeStruct(density.shape, F32),

time: 48.4 us -> 48.3 us (level)
  no operation moved by 1% of the time
where the time goes in v10:
time: 48.3 us; the launch traced here: 48.1 us
  blocking collectives  43.7 us (90%)
  Pallas kernels  4.41 us (9%)
    all_to_all x2, blocking collectives, exchange(): whole = lax.all_to_all(whole, ('core', 'gz', 'x'), 0, 0, tiled=True)  43.7 us
    pallas_call x1, Pallas kernels, on_device(): pl.pallas_call(forward_x, out_shape=(message, factors, factors), in_specs...  1.81 us
    pallas_call x1, Pallas kernels, on_device(): pl.pallas_call(backward_x, out_shape=jax.ShapeDtypeStruct(density.shape,...  1.42 us
    pallas_call x1, Pallas kernels, on_device(): pl.pallas_call(middle, out_shape=message, in_specs=[vmem] * 5, out_specs=...  1.19 us

profile of v10, /device:TPU:1, one launch (start us, length us, event | category | flops | bytes accessed | tf_op | source)
XLA Modules:
  0.0 48.1 jit_solution(7448067142846119480)
XLA Ops:
  0.0 1.8 %shard_map.55 = (f32[1152,128]{1,0:T(8,128)S(1)}, f32[24,384]{1,0:T(8,128)S(1)}, f32[24,384]{1,0:T(8,128)S(1)}) custom-call(f32[8,15488]{1,0:T(8,128)} %x_ref.1, bf16[2,2,192,256]{3,2,1,0:T(8,128)(2,1)} %constant.8.clone.table_ref), custom_call_target="tpu_custom_call" | custom-call | tf_op jit(solution)/shard_map/pallas_call | solution.py:369
  1.8 0.0 copy-start.1
  1.8 0.0 copy-start.2
  1.8 25.4 %all_to_all.10 = f32[128,1,1152]{2,1,0:T(1,128)S(1)} all-to-all(f32[128,1,1152]{2,1,0:T(1,128)S(1)} %bitcast.7), channel_id=1, replica_groups=mesh['gz'=16,'x'=4,'core'=2] {'core','gz','x'}, dimensions={0} | all-to-all | bytes 1179648 | tf_op jit(solution)/shard_map/all_to_all | solution.py:350
  27.3 0.0 copy-done.1
  27.3 0.0 copy-done.2
  27.3 1.2 %shard_map.56 = f32[1152,128]{1,0:T(8,128)S(1)} custom-call(f32[1152,128]{1,0:T(8,128)S(1)} %bitcast.4, bf16[2,2,256,256]{3,2,1,0:T(8,128)(2,1)S(1)} %copy-done.1, bf16[2,2,256,256]{3,2,1,0:T(8,128)(2,1)S(1)} %copy-done.2, f32[24,384]{1,0:T(8,128)S(1)} %get-tuple-element.9.decay_ref, f32[24,384]{1,0:T(8,128)S(1)} %get-tuple-element.10.scale_ref), custom_call_target="tpu_custom_call" | custom-call | tf_op jit(solution)/shard_map/pallas_call | solution.py:382
  28.5 0.0 copy-start
  28.5 18.2 %all_to_all.11 = f32[128,1,1152]{2,1,0:T(1,128)S(1)} all-to-all(f32[128,1,1152]{2,1,0:T(1,128)S(1)} %bitcast.5), channel_id=1, replica_groups=mesh['gz'=16,'x'=4,'core'=2] {'core','gz','x'}, dimensions={0} | all-to-all | bytes 1179648 | tf_op jit(solution)/shard_map/all_to_all | solution.py:350
  46.7 0.0 copy-done
  46.7 1.4 %shard_map.57 = f32[8,15488]{1,0:T(8,128)} custom-call(f32[1152,128]{1,0:T(8,128)S(1)} %bitcast.6, bf16[2,2,256,256]{3,2,1,0:T(8,128)(2,1)S(1)} %copy-done), custom_call_target="tpu_custom_call" | custom-call | tf_op jit(solution)/shard_map/pallas_call | solution.py:389
Async XLA Ops:
  1.8 25.5 %copy-start.1 = (bf16[2,2,256,256]{3,2,1,0:T(8,128)(2,1)S(1)}, bf16[2,2,256,256]{3,2,1,0:T(8,128)(2,1)}, u32[]{:S(2)}) copy-start(bf16[2,2,256,256]{3,2,1,0:T(8,128)(2,1)} %constant.10.clone.turned_ref) | copy-start | bytes 1572868
  1.8 25.5 %copy-start.2 = (bf16[2,2,256,256]{3,2,1,0:T(8,128)(2,1)S(1)}, bf16[2,2,256,256]{3,2,1,0:T(8,128)(2,1)}, u32[]{:S(2)}) copy-start(bf16[2,2,256,256]{3,2,1,0:T(8,128)(2,1)} %constant.9.clone.table_ref) | copy-start | bytes 1572868
  28.5 18.2 %copy-start = (bf16[2,2,256,256]{3,2,1,0:T(8,128)(2,1)S(1)}, bf16[2,2,256,256]{3,2,1,0:T(8,128)(2,1)}, u32[]{:S(2)}) copy-start(bf16[2,2,256,256]{3,2,1,0:T(8,128)(2,1)} %constant.11.clone.table_ref) | copy-start | bytes 1572868

commit v11 on v10

--- a/solution.py
+++ b/solution.py
@@ -29,7 +29,7 @@
 CHUNK = PAD // GY
 PITCH = PLANES + 1
 BLOCKS = (0, 16, 32, CHUNK)
-PARTS = (0, 24, ROWS)
+PARTS = (0, ROWS)
 OWN = 3
 PEERS = GZ * GY
 SEND = PEERS * OWN * TILES

time: 48.3 us -> 48.3 us (level)
  no operation moved by 1% of the time
where the time goes in v11:
time: 48.3 us; the launch traced here: 48.2 us
  blocking collectives  43.7 us (90%)
  Pallas kernels  4.41 us (9%)
    all_to_all x2, blocking collectives, exchange(): whole = lax.all_to_all(whole, ('core', 'gz', 'x'), 0, 0, tiled=True)  43.7 us
    pallas_call x1, Pallas kernels, on_device(): pl.pallas_call(forward_x, out_shape=(message, factors, factors), in_specs...  1.81 us
    pallas_call x1, Pallas kernels, on_device(): pl.pallas_call(backward_x, out_shape=jax.ShapeDtypeStruct(density.shape,...  1.42 us
    pallas_call x1, Pallas kernels, on_device(): pl.pallas_call(middle, out_shape=message, in_specs=[vmem] * 5, out_specs=...  1.19 us

profile of v11, /device:TPU:1, one launch (start us, length us, event | category | flops | bytes accessed | tf_op | source)
XLA Modules:
  0.0 48.2 jit_solution(17757738692886863290)
XLA Ops:
  0.0 1.8 %shard_map.55 = (f32[1152,128]{1,0:T(8,128)S(1)}, f32[24,384]{1,0:T(8,128)S(1)}, f32[24,384]{1,0:T(8,128)S(1)}) custom-call(f32[8,15488]{1,0:T(8,128)} %x_ref.1, bf16[2,2,192,256]{3,2,1,0:T(8,128)(2,1)} %constant.8.clone.table_ref), custom_call_target="tpu_custom_call" | custom-call | tf_op jit(solution)/shard_map/pallas_call | solution.py:369
  1.8 0.0 copy-start.1
  1.8 0.0 copy-start.2
  1.8 25.5 %all_to_all.10 = f32[128,1,1152]{2,1,0:T(1,128)S(1)} all-to-all(f32[128,1,1152]{2,1,0:T(1,128)S(1)} %bitcast.7), channel_id=1, replica_groups=mesh['gz'=16,'x'=4,'core'=2] {'core','gz','x'}, dimensions={0} | all-to-all | bytes 1179648 | tf_op jit(solution)/shard_map/all_to_all | solution.py:350
  27.3 0.0 copy-done.1
  27.3 0.0 copy-done.2
  27.3 1.2 %shard_map.56 = f32[1152,128]{1,0:T(8,128)S(1)} custom-call(f32[1152,128]{1,0:T(8,128)S(1)} %bitcast.4, bf16[2,2,256,256]{3,2,1,0:T(8,128)(2,1)S(1)} %copy-done.1, bf16[2,2,256,256]{3,2,1,0:T(8,128)(2,1)S(1)} %copy-done.2, f32[24,384]{1,0:T(8,128)S(1)} %get-tuple-element.9.decay_ref, f32[24,384]{1,0:T(8,128)S(1)} %get-tuple-element.10.scale_ref), custom_call_target="tpu_custom_call" | custom-call | tf_op jit(solution)/shard_map/pallas_call | solution.py:382
  28.5 0.0 copy-start
  28.5 18.2 %all_to_all.11 = f32[128,1,1152]{2,1,0:T(1,128)S(1)} all-to-all(f32[128,1,1152]{2,1,0:T(1,128)S(1)} %bitcast.5), channel_id=1, replica_groups=mesh['gz'=16,'x'=4,'core'=2] {'core','gz','x'}, dimensions={0} | all-to-all | bytes 1179648 | tf_op jit(solution)/shard_map/all_to_all | solution.py:350
  46.7 0.0 copy-done
  46.7 1.4 %shard_map.57 = f32[8,15488]{1,0:T(8,128)} custom-call(f32[1152,128]{1,0:T(8,128)S(1)} %bitcast.6, bf16[2,2,256,256]{3,2,1,0:T(8,128)(2,1)S(1)} %copy-done), custom_call_target="tpu_custom_call" | custom-call | tf_op jit(solution)/shard_map/pallas_call | solution.py:389
Async XLA Ops:
  1.8 25.5 %copy-start.1 = (bf16[2,2,256,256]{3,2,1,0:T(8,128)(2,1)S(1)}, bf16[2,2,256,256]{3,2,1,0:T(8,128)(2,1)}, u32[]{:S(2)}) copy-start(bf16[2,2,256,256]{3,2,1,0:T(8,128)(2,1)} %constant.10.clone.turned_ref) | copy-start | bytes 1572868
  1.8 25.5 %copy-start.2 = (bf16[2,2,256,256]{3,2,1,0:T(8,128)(2,1)S(1)}, bf16[2,2,256,256]{3,2,1,0:T(8,128)(2,1)}, u32[]{:S(2)}) copy-start(bf16[2,2,256,256]{3,2,1,0:T(8,128)(2,1)} %constant.9.clone.table_ref) | copy-start | bytes 1572868
  28.5 18.2 %copy-start = (bf16[2,2,256,256]{3,2,1,0:T(8,128)(2,1)S(1)}, bf16[2,2,256,256]{3,2,1,0:T(8,128)(2,1)}, u32[]{:S(2)}) copy-start(bf16[2,2,256,256]{3,2,1,0:T(8,128)(2,1)} %constant.11.clone.table_ref) | copy-start | bytes 1572868
